TPU v7x, 32 devices: a whole 2x2x4 slice. The times are simulated.
32 devices in a mesh: seq: 8 (over y, x, core), head: 4 (over z).
Axes of the slice: x: 2, y: 2, z: 4, core: 2. Of those that a mesh axis runs over, the one named last changes fastest.
Arguments:
- video_rows: bfloat16 [4096, 5120], P('seq'), may hold values from -6 to 6
- context: bfloat16 [512, 5120], P('seq'), may hold values from -6 to 6
- valid_length: int32 [1], replicated, may hold values from 64 to 512
- timestep: int32 [1], replicated, may hold values from 0 to 999
- query_weight: bfloat16 [5120, 1024], P('seq', 'head'), may hold values from -0.078125 to 0.078125
- key_weight: bfloat16 [5120, 1024], P('seq', 'head'), may hold values from -0.078125 to 0.078125
- value_weight: bfloat16 [5120, 1024], P('seq', 'head'), may hold values from -0.078125 to 0.078125
- out_weight: bfloat16 [1024, 5120], P('head', 'seq'), may hold values from -0.1875 to 0.1875
- query_gain: float32 [1024], P('head'), may hold values from 0.5 to 15
- key_gain: float32 [1024], P('head'), may hold values from 0.5 to 15
- time_weight: bfloat16 [2, 256, 5120], P(None, None, 'head'), may hold values from -0.375 to 0.375
- modulation: float32 [2, 5120], P(None, 'head'), may hold values from -3 to 3
Outputs:
- residual_out: bfloat16 [4096, 5120], P('seq', 'head')
- modulated: bfloat16 [4096, 5120], P('seq', 'head')
Inputs may be any that keep to these rules, and one draw needn't show every extreme that they name: `valid_length`: text positions at or beyond it are padding.
All inputs are finite; a program needn't handle non-finite values.
Results may differ from a plain program's by a relative error of at most 0.0065.
The roundings to bfloat16 on the way count: a program that leaves them out, or rounds other values in their place, can miss the bound.
Values may be sent and summed in bfloat16 or wider, within the bound.
A program may use at most 64 MiB of HBM per device.

v0:
```python
import functools

import jax
import jax.numpy as jnp
from jax import lax
from jax.experimental import pallas as pl
from jax.experimental.pallas import tpu as pltpu
from jax.sharding import PartitionSpec as P

HD = 128
FREQ = 256
LANES = 128
F32 = jnp.float32
BF16 = jnp.bfloat16
MESH_ID = pl.DeviceIdType.MESH


def flip(index, mask):
    bit = 1
    while bit <= mask:
        if mask & bit:
            index = index + bit - 2 * bit * ((index // bit) % 2)
        bit *= 2
    return index


def rows_to_lanes(column, tall):
    return jnp.transpose(jnp.broadcast_to(column, (tall, LANES)))[:8]


def body(
    n_seq, n_head, chunks, sliced,
    valid, video, ctx, qw, kw, vw, ow, qg, kg, act, tw, mod, *rest,
):
    if sliced:
        steps(n_seq, n_head, chunks, valid, video, ctx, qw, kw, vw, ow, qg, kg, act, tw, mod, *rest)
    else:
        steps(
            n_seq, n_head, chunks, valid, video, ctx, qw, kw, vw, ow, qg, kg, act, tw, mod,
            None, *rest,
        )


def steps(
    n_seq, n_head, chunks,
    valid, video, ctx, qw, kw, vw, ow, qg, kg, act, tw, mod, vpart,
    resid_out, mod_out,
    vid, normed, ctxg, qwg, part, pair, rsg, own_kv, kvg, spread, owg, attg,
    queries, qsq, ksq, stat, shsc,
    vid_sem, loc_sem, ctx_s, ctx_r, qw_s, qw_r, pr_s, pr_r, rs_s, rs_r, kv_s, kv_r,
    sp_s, sp_r, oz_s, oz_r, og_s, og_r, ksq_s, ksq_r, qsq_s, qsq_r, at_s, at_r, st_s, st_r,
):
    s = lax.axis_index("seq")
    z = lax.axis_index("head")
    core = s % 2
    chip = s // 2
    n_chip = n_seq // 2
    ratio = n_seq // n_head
    tok, width = vid.shape
    depth = qw.shape[0]
    att = qw.shape[1]
    text = ctxg.shape[1]
    sent = []

    def to_seq(k):
        return (flip(s, k), z)

    def to_head(k):
        return (s, flip(z, k))

    def remote(src, dst, ssem, rsem, dev):
        return pltpu.make_async_remote_copy(
            src_ref=src, dst_ref=dst, send_sem=ssem, recv_sem=rsem,
            device_id=dev, device_id_type=MESH_ID,
        )

    def push(src, dst, ssem, rsem, dev):
        copy = remote(src, dst, ssem, rsem, dev)
        copy.start()
        sent.append(copy)

    def arrived(dst, ssem, rsem, dev):
        remote(dst, dst, ssem, rsem, dev).wait_recv()

    def gather_start(slot, ssem, rsem):
        for k in range(2, n_seq, 2):
            push(slot(s), slot(s), ssem.at[k], rsem.at[k], to_seq(k))
        push(slot(s), slot(s), ssem.at[1], rsem.at[1], to_seq(1))

    def gather_relay(slot, ssem, rsem):
        for k in range(2, n_seq, 2):
            arrived(slot(flip(s, k)), ssem.at[k], rsem.at[k], to_seq(k))
            push(slot(flip(s, k)), slot(flip(s, k)), ssem.at[k + 1], rsem.at[k + 1], to_seq(1))

    def gather_end(slot, ssem, rsem):
        for k in range(1, n_seq, 2):
            arrived(slot(flip(s, k)), ssem.at[k], rsem.at[k], to_seq(1))

    load = pltpu.make_async_copy(video, vid, vid_sem)
    load.start()

    def ctx_piece(p):
        if len(ctx.shape) == 3:
            return ctx.at[p]
        return ctx.at[:, pl.ds(pl.multiple_of(p * depth, depth), depth)]


    def qw_slot(p):
        return qwg.at[pl.ds(pl.multiple_of(p * depth, depth), depth), :]

    def qw_half(i, p):
        rows = depth // 2
        return qwg.at[pl.ds(pl.multiple_of(p * depth + i * rows, rows), rows), :]

    own_qw = pltpu.make_async_copy(qw, qw_slot(s), loc_sem.at[0])
    own_qw.start()
    own_ctx = pltpu.make_async_copy(ctx_piece(s), ctxg.at[s], loc_sem.at[1])
    own_ctx.start()
    piece = ow.shape[0] // n_seq

    def ow_piece(p):
        return pl.ds(pl.multiple_of(p * piece, piece), piece)

    own_spread = pltpu.make_async_copy(ow.at[ow_piece(s), :], spread.at[s], loc_sem.at[2])
    own_spread.start()

    barrier = pltpu.get_barrier_semaphore()
    for k in range(1, n_seq):
        pl.semaphore_signal(barrier, inc=1, device_id=to_seq(k), device_id_type=MESH_ID)
    for k in range(1, n_head):
        pl.semaphore_signal(barrier, inc=1, device_id=to_head(k), device_id_type=MESH_ID)
    pl.semaphore_wait(barrier, n_seq + n_head - 2)

    for k in range(1, n_seq):
        push(ctx_piece(flip(s, k)), ctxg.at[s], ctx_s.at[k], ctx_r.at[k], to_seq(k))
    own_qw.wait()
    gather_start(functools.partial(qw_half, 0), qw_s.at[0], qw_r.at[0])

    load.wait()
    strip = 16

    @pl.loop(0, tok // strip)
    def _(i):
        at = pl.ds(pl.multiple_of(i * strip, strip), strip)
        rows = vid[at, :].astype(F32)
        mean = jnp.mean(rows, axis=-1, keepdims=True)
        centred = rows - mean
        spread_ = jnp.mean(centred * centred, axis=-1, keepdims=True)
        normed[at, :] = (centred / jnp.sqrt(spread_ + 1e-06)).astype(BF16)

    own_ctx.wait()
    for k in range(1, n_seq):
        arrived(ctxg.at[flip(s, k)], ctx_s.at[k], ctx_r.at[k], to_seq(k))
    source = ctxg[...].reshape(n_seq * text, depth)
    keys = jnp.dot(source, kw[...], preferred_element_type=F32)
    part[:, :, :, :att] = keys.reshape(n_chip, 2, text, att)
    values = jnp.dot(source, vw[...], preferred_element_type=F32)
    part[:, :, :, att:] = values.reshape(n_chip, 2, text, att)
    push(part.at[:, 1 - core], pair, pr_s, pr_r, to_seq(1))

    for i in range(2):
        shsc[i] = mod[i : i + 1, :] + jnp.dot(act[...], tw[i], preferred_element_type=F32)[:8]

    arrived(pair, pr_s, pr_r, to_seq(1))
    for c in range(n_chip):
        rsg[0, c] = part[c, core] + pair[c]
    for k in range(1, n_chip):
        push(
            rsg.at[0, flip(chip, k)], rsg.at[k, chip], rs_s.at[k], rs_r.at[k], to_seq(2 * k)
        )

    gather_start(functools.partial(qw_half, 1), qw_s.at[1], qw_r.at[1])
    for k in range(1, n_seq):
        push(ow.at[ow_piece(flip(s, k)), :], spread.at[s], sp_s.at[k], sp_r.at[k], to_seq(k))

    for i in range(2):
        gather_relay(functools.partial(qw_half, i), qw_s.at[i], qw_r.at[i])
    for i in range(2):
        gather_end(functools.partial(qw_half, i), qw_s.at[i], qw_r.at[i])
    queries[...] = jnp.dot(normed[...], qwg[...], preferred_element_type=F32)
    q_sum = jnp.sum(queries[...] * queries[...], axis=1, keepdims=True)
    qsq[0] = rows_to_lanes(q_sum, tok)

    total = rsg[0, chip]
    for k in range(1, n_chip):
        arrived(rsg.at[k, flip(chip, k)], rs_s.at[k], rs_r.at[k], to_seq(2 * k))
        total = total + rsg[k, flip(chip, k)]
    key_rows = total[:, :att]
    k_sum = jnp.sum(key_rows * key_rows, axis=1, keepdims=True)
    ksq[0] = jnp.broadcast_to(k_sum, (text, LANES))
    for k in range(1, n_head):
        push(ksq.at[0], ksq.at[k], ksq_s.at[k], ksq_r.at[k], to_head(k))
    for k in range(1, n_head):
        push(qsq.at[0], qsq.at[k], qsq_s.at[k], qsq_r.at[k], to_head(k))
    for k in range(1, n_head):
        arrived(ksq.at[k], ksq_s.at[k], ksq_r.at[k], to_head(k))
    k_mean = jnp.sum(ksq[...], axis=0)[:, :1] / (att * n_head)
    own_kv[:, :att] = (key_rows / jnp.sqrt(k_mean + 1e-06) * kg[...]).astype(BF16)
    own_kv[:, att:] = total[:, att:].astype(BF16)
    kvg[s] = own_kv[...]

    def kv_slot(p):
        return kvg.at[p]

    gather_start(kv_slot, kv_s, kv_r)

    own_spread.wait()
    for k in range(1, n_seq):
        arrived(spread.at[flip(s, k)], sp_s.at[k], sp_r.at[k], to_seq(k))

    def own_cols(zz):
        return pl.ds(zz * ratio, ratio)

    own_ow = pltpu.make_async_copy(
        spread.at[own_cols(z)], owg.at[:, z, ow_piece(s), :], loc_sem.at[3]
    )
    own_ow.start()
    for k in range(1, n_head):
        push(
            spread.at[own_cols(flip(z, k))], owg.at[:, z, ow_piece(s), :],
            oz_s.at[k], oz_r.at[k], to_head(k),
        )

    for k in range(1, n_head):
        arrived(qsq.at[k], qsq_s.at[k], qsq_r.at[k], to_head(k))
    q_lane = jnp.sum(qsq[...], axis=0)
    q_mean = jnp.transpose(q_lane)[:, :1] / (att * n_head)
    q_normed = (queries[...] / jnp.sqrt(q_mean + 1e-06) * qg[...]).astype(BF16)

    own_ow.wait()
    for k in range(1, n_head):
        arrived(owg.at[:, flip(z, k), ow_piece(s), :], oz_s.at[k], oz_r.at[k], to_head(k))

    def ow_slot(p):
        return owg.at[:, :, ow_piece(p), :]

    gather_relay(kv_slot, kv_s, kv_r)
    gather_start(ow_slot, og_s, og_r)
    gather_end(kv_slot, kv_s, kv_r)

    every = kvg[...].reshape(n_seq * text, 2 * att)
    all_text = n_seq * text
    seen = lax.broadcasted_iota(jnp.int32, (1, all_text), 1) < valid[0]
    step = tok // chunks
    for c in range(chunks):
        at = slice(c * step, (c + 1) * step)
        for h in range(att // HD):
            lanes = slice(h * HD, (h + 1) * HD)
            scores = lax.dot_general(
                q_normed[at, lanes], every[:, lanes], (((1,), (1,)), ((), ())),
                preferred_element_type=F32,
            ) * HD ** (-0.5)
            scores = jnp.where(seen, scores, F32(-1e30))
            shifted = jnp.exp(scores - jnp.max(scores, axis=-1, keepdims=True))
            weights = (shifted / jnp.sum(shifted, axis=-1, keepdims=True)).astype(BF16)
            attg[0, at, lanes] = jnp.dot(
                weights, every[:, att + h * HD : att + (h + 1) * HD],
                preferred_element_type=F32,
            ).astype(BF16)
        for k in range(1, n_head):
            push(
                attg.at[0, at], attg.at[k, at],
                at_s.at[c, k], at_r.at[c, k], to_head(k),
            )
    gather_relay(ow_slot, og_s, og_r)
    gather_end(ow_slot, og_s, og_r)

    cols = owg.shape[3]
    part_width = mod_out.shape[1]
    sums = []
    squares = []
    for c in range(chunks):
        at = slice(c * step, (c + 1) * step)
        for k in range(1, n_head):
            arrived(attg.at[k, at], at_s.at[c, k], at_r.at[c, k], to_head(k))
        row_sum = jnp.zeros((step, 1), F32)
        row_sq = jnp.zeros((step, 1), F32)
        for j in range(ratio):
            here = slice(j * cols, (j + 1) * cols)
            projected = jnp.dot(attg[0, at], owg[j, z], preferred_element_type=F32)
            for k in range(1, n_head):
                projected = projected + jnp.dot(
                    attg[k, at], owg[j, flip(z, k)], preferred_element_type=F32
                )
            if vpart is None:
                mine = vid[at, pl.ds(pl.multiple_of(z * part_width + j * cols, LANES), cols)]
            else:
                mine = vpart[at, here]
            rounded = (mine.astype(F32) + projected).astype(BF16)
            resid_out[at, here] = rounded
            wide = rounded.astype(F32)
            row_sum = row_sum + jnp.sum(wide, axis=1, keepdims=True)
            row_sq = row_sq + jnp.sum(wide * wide, axis=1, keepdims=True)
        sums.append(row_sum)
        squares.append(row_sq)
    stat[0, :8] = rows_to_lanes(jnp.concatenate(sums, axis=0), tok)
    stat[0, 8:] = rows_to_lanes(jnp.concatenate(squares, axis=0), tok)
    for k in range(1, n_head):
        push(stat.at[0], stat.at[k], st_s.at[k], st_r.at[k], to_head(k))
    for k in range(1, n_head):
        arrived(stat.at[k], st_s.at[k], st_r.at[k], to_head(k))
    both = jnp.sum(stat[...], axis=0) / (mod_out.shape[1] * n_head)
    mean2 = both[:8]
    inverse = 1.0 / jnp.sqrt(both[8:] - mean2 * mean2 + 1e-06)
    mean_col = jnp.transpose(mean2)[:, :1]
    inv_col = jnp.transpose(inverse)[:, :1]
    for c in range(chunks):
        at = slice(c * step, (c + 1) * step)
        wide = resid_out[at, :].astype(F32)
        mod_out[at, :] = (
            (wide - mean_col[at]) * inv_col[at] * (1.0 + shsc[1, :1, :]) + shsc[0, :1, :]
        ).astype(BF16)
    for copy in sent:
        copy.wait_send()


def on_device(
    n_seq,
    n_head,
    video_rows,
    context,
    valid_length,
    timestep,
    query_weight,
    key_weight,
    value_weight,
    out_weight,
    query_gain,
    key_gain,
    time_weight,
    modulation,
):
    tok, width = video_rows.shape
    text = context.shape[0]
    depth, att = query_weight.shape
    cols = out_weight.shape[1]
    part_width = modulation.shape[1]
    ratio = n_seq // n_head
    n_chip = n_seq // 2
    chunks = 4
    piece = out_weight.shape[0] // n_seq
    half = FREQ // 2
    freqs = jnp.exp(-jnp.log(10000.0) * jnp.arange(half, dtype=F32) / half)
    angles = timestep[0].astype(F32) * freqs
    embedding = jnp.concatenate([jnp.cos(angles), jnp.sin(angles)])
    act = jnp.broadcast_to(jax.nn.silu(embedding).astype(BF16)[None, :], (16, FREQ))
    blocks = context
    if depth % LANES:
        blocks = context.reshape(text, n_seq, depth).transpose(1, 0, 2)
    sliced = part_width % LANES != 0 or cols % LANES != 0
    extra = []
    if sliced:
        extra.append(
            lax.dynamic_slice_in_dim(
                video_rows, lax.axis_index("head") * part_width, part_width, 1
            )
        )
    vmem = pl.BlockSpec(memory_space=pltpu.VMEM)
    dma = pltpu.SemaphoreType.DMA
    seq_sems = [dma((n_seq,))] * 2
    head_sems = [dma((n_head,))] * 2
    return pl.pallas_call(
        functools.partial(body, n_seq, n_head, chunks, sliced),
        out_shape=[jax.ShapeDtypeStruct((tok, part_width), BF16)] * 2,
        in_specs=[
            pl.BlockSpec(memory_space=pltpu.SMEM),
            pl.BlockSpec(memory_space=pl.ANY),
        ]
        + [vmem] * (10 + len(extra)),
        out_specs=[vmem] * 2,
        scratch_shapes=[
            pltpu.VMEM((tok, width), BF16),
            pltpu.VMEM((tok, width), BF16),
            pltpu.VMEM((n_seq, text, depth), BF16),
            pltpu.VMEM((n_seq * depth, att), BF16),
            pltpu.VMEM((n_chip, 2, text, 2 * att), F32),
            pltpu.VMEM((n_chip, text, 2 * att), F32),
            pltpu.VMEM((n_chip, n_chip, text, 2 * att), F32),
            pltpu.VMEM((text, 2 * att), BF16),
            pltpu.VMEM((n_seq, text, 2 * att), BF16),
            pltpu.VMEM((n_seq, piece, cols), BF16),
            pltpu.VMEM((ratio, n_head, out_weight.shape[0], cols), BF16),
            pltpu.VMEM((n_head, tok, att), BF16),
            pltpu.VMEM((tok, att), F32),
            pltpu.VMEM((n_head, 8, tok), F32),
            pltpu.VMEM((n_head, text, LANES), F32),
            pltpu.VMEM((n_head, 16, tok), F32),
            pltpu.VMEM((2, 8, part_width), F32),
            dma,
            dma((4,)),
            *seq_sems,
            *[dma((2, n_seq))] * 2,
            dma,
            dma,
            *[dma((n_chip,))] * 2,
            *seq_sems,
            *seq_sems,
            *head_sems,
            *seq_sems,
            *head_sems,
            *head_sems,
            *[dma((chunks, n_head))] * 2,
            *head_sems,
        ],
        compiler_params=pltpu.CompilerParams(
            collective_id=0, has_side_effects=True, vmem_limit_bytes=60 * 1024 * 1024
        ),
    )(
        valid_length,
        video_rows,
        blocks,
        query_weight,
        key_weight,
        value_weight,
        out_weight,
        query_gain[None, :],
        key_gain[None, :],
        act,
        time_weight,
        modulation,
        *extra,
    )


def solution(mesh):
    in_specs = (
        P("seq", None),
        P("seq", None),
        P(),
        P(),
        P("seq", "head"),
        P("seq", "head"),
        P("seq", "head"),
        P("head", "seq"),
        P("head"),
        P("head"),
        P(None, None, "head"),
        P(None, "head"),
    )
    out_specs = (P("seq", "head"), P("seq", "head"))
    return jax.shard_map(
        functools.partial(on_device, mesh.shape["seq"], mesh.shape["head"]),
        mesh=mesh, in_specs=in_specs, out_specs=out_specs, check_vma=False,
    )
```

profile of v0, /device:TPU:0, one launch (start us, length us, event | category | flops | bytes accessed | tf_op | source)
XLA Modules:
  0.0 97.7 jit_solution(12996414486646224320)
XLA Ops:
  2.0 0.6 broadcast_in_dim.14.act
  2.6 91.4 %shard_map.131 = (bf16[512,1280]{1,0:T(8,128)(2,1)}, bf16[512,1280]{1,0:T(8,128)(2,1)}) custom-call(s32[1]{0:T(128)S(6)} %copy.16.valid, bf16[512,5120]{1,0:T(8,128)(2,1)} %video.1, bf16[64,5120]{1,0:T(8,128)(2,1)} %ctx.1, bf16[640,256]{1,0:T(8,128)(2,1)} %qw.1, bf16[640,256]{1,0:T(8,128)(2,1)} %kw.1, bf16[640,256]{1,0:T(8,128)(2,1)} %vw.1, ...), custom_call_target="tpu_custom_call" | custom-call | tf_op jit(solution)/shard_map/pallas_call | solution.py:362
  94.1 0.0 copy-start
  94.1 2.6 %copy.18 = bf16[512,1280]{1,0:T(8,128)(2,1)} copy(bf16[512,1280]{1,0:T(8,128)(2,1)} %get-tuple-element.6) | data formatting | bytes 2621440
  96.6 0.0 copy-done
  96.6 1.1 %copy.19 = bf16[512,1280]{1,0:T(8,128)(2,1)} copy(bf16[512,1280]{1,0:T(8,128)(2,1)S(1)} %copy-done) | data formatting | bytes 2621440
  (2 shorter events, 0.1 us)
Async XLA Ops:
  94.1 2.6 %copy-start = (bf16[512,1280]{1,0:T(8,128)(2,1)S(1)}, bf16[512,1280]{1,0:T(8,128)(2,1)}, u32[]{:S(2)}) copy-start(bf16[512,1280]{1,0:T(8,128)(2,1)} %get-tuple-element.7) | copy-start | bytes 3932164
where the time goes:
time: 97.9 us; the launch traced here: 97.7 us
  Pallas kernels  91.4 us (93%)
  local copies, waits for them, and re-layouts  4.24 us (4%)
  between operations  1.95 us (2%)
    pallas_call x1, Pallas kernels, on_device(): pl.pallas_call(functools.partial(body, n_seq, n_head, chunks, sliced), ou...  91.4 us
    unnamed x4, local copies, waits for them, and re-layouts  3.62 us

commit v1 on v0

v1 whole, which is shorter than its diff:
```python
import functools

import jax
import jax.numpy as jnp
from jax import lax
from jax.experimental import pallas as pl
from jax.experimental.pallas import tpu as pltpu
from jax.sharding import PartitionSpec as P

HD = 128
FREQ = 256
LANES = 128
F32 = jnp.float32
BF16 = jnp.bfloat16
MESH_ID = pl.DeviceIdType.MESH


def flip(index, mask):
    bit = 1
    while bit <= mask:
        if mask & bit:
            index = index + bit - 2 * bit * ((index // bit) % 2)
        bit *= 2
    return index


def bits_of(mask):
    return [1 << b for b in range(mask.bit_length()) if mask >> b & 1]


def last_bit(half, mask):
    return bits_of(mask)[-1] if half == 0 else bits_of(mask)[0]


def by_hops(n_seq):
    return sorted(range(2, n_seq, 2), key=lambda k: (len(bits_of(k)), k))


def column_to_row(column):
    tall = column.shape[0]
    wide = -(-tall // LANES) * LANES
    if wide > tall:
        column = jnp.concatenate([column, jnp.zeros((wide - tall, 1), F32)], axis=0)
    return jnp.transpose(jnp.broadcast_to(column, (wide, LANES)))[:1]


def row_to_column(row, tall):
    return jnp.transpose(jnp.broadcast_to(row, (LANES, row.shape[1])))[:tall, :1]


def body(n_seq, n_head, chunks, sliced, *refs):
    if sliced:
        steps(n_seq, n_head, chunks, *refs)
    else:
        steps(n_seq, n_head, chunks, *refs[:12], None, *refs[12:])


def steps(
    n_seq, n_head, chunks,
    valid, video, ctx, qw, kw, vw, ow, qg, kg, act, tw_hbm, mod, vpart,
    resid_out, mod_out,
    vid, normed, ctxv, ctxg, qwg, kvw, cks, ckr, cvs, cvr, kall, vall, spread, owg, attg,
    queries, qsq, ksq, stat, shsc, tw,
    loc_sem, ctx_s, ctx_r, qw_s, qw_r, w_s, w_r, ck_s, ck_r, cv_s, cv_r, k_s, k_r, v_s, v_r,
    sp_s, sp_r, oz_s, oz_r, og_s, og_r, ksq_s, ksq_r, qsq_s, qsq_r, at_s, at_r, st_s, st_r,
):
    s = lax.axis_index("seq")
    z = lax.axis_index("head")
    core = s % 2
    chip = s // 2
    n_chip = n_seq // 2
    ratio = n_seq // n_head
    tok, width = vid.shape
    depth = qw.shape[0]
    att = qw.shape[1]
    text = ctx.shape[0]
    pair = 2 * depth
    sent = []
    masks = by_hops(n_seq)
    chip_bits = [k for k in masks if len(bits_of(k)) == 1]

    def to_seq(k):
        return (flip(s, k), z)

    def to_head(k):
        return (s, flip(z, k))

    def remote(src, dst, ssem, rsem, dev):
        return pltpu.make_async_remote_copy(
            src_ref=src, dst_ref=dst, send_sem=ssem, recv_sem=rsem,
            device_id=dev, device_id_type=MESH_ID,
        )

    def push(src, dst, ssem, rsem, dev):
        copy = remote(src, dst, ssem, rsem, dev)
        copy.start()
        sent.append((None, copy))

    def arrived(dst, ssem, rsem, dev):
        remote(dst, dst, ssem, rsem, dev).wait_recv()

    def gather_own(slot, half, bits, ssem, rsem):
        for b in bits:
            push(slot(half, s), slot(half, s), ssem.at[half, b], rsem.at[half, b], to_seq(b))

    def gather_core(slot, half, ssem, rsem):
        push(slot(half, s), slot(half, s), ssem.at[half, 1], rsem.at[half, 1], to_seq(1))

    def gather_relay(slot, half, k, ssem, rsem):
        here = slot(half, flip(s, k))
        arrived(here, ssem.at[half, k], rsem.at[half, k], to_seq(last_bit(half, k)))
        for b in chip_bits:
            if not k & b and last_bit(half, k | b) == b:
                push(here, here, ssem.at[half, k | b], rsem.at[half, k | b], to_seq(b))
        push(here, here, ssem.at[half, k + 1], rsem.at[half, k + 1], to_seq(1))

    def gather_end(slot, half, k, ssem, rsem):
        here = slot(half, flip(s, k + 1))
        arrived(here, ssem.at[half, k + 1], rsem.at[half, k + 1], to_seq(1))

    barrier = pltpu.get_barrier_semaphore()
    for k in range(1, n_seq):
        pl.semaphore_signal(barrier, inc=1, device_id=to_seq(k), device_id_type=MESH_ID)
    for k in range(1, n_head):
        pl.semaphore_signal(barrier, inc=1, device_id=to_head(k), device_id_type=MESH_ID)

    def half_rows(half, p):
        rows = depth // 2
        return qwg.at[pl.ds(pl.multiple_of(p * depth + half * rows, rows), rows), :]

    def load(src, dst, i):
        copy = pltpu.make_async_copy(src, dst, loc_sem.at[i])
        copy.start()
        return copy

    piece = ow.shape[0] // n_seq

    def ow_piece(p):
        return pl.ds(pl.multiple_of(p * piece, piece), piece)

    own_ctx = load(ctx, ctxv, 0)
    own_qw = load(qw, qwg.at[pl.ds(pl.multiple_of(s * depth, depth), depth), :], 1)
    own_kw = load(kw, kvw.at[core, :, :att], 2)
    own_vw = load(vw, kvw.at[core, :, att:], 3)
    own_vid = load(video, vid, 4)
    own_spread = load(ow.at[ow_piece(s), :], spread.at[s], 5)
    own_tw = load(tw_hbm, tw, 6)
    pl.semaphore_wait(barrier, n_seq + n_head - 2)

    def ctx_cols(p):
        return pl.ds(pl.multiple_of(p * pair, pair), pair)

    own_ctx.wait()
    for k in masks:
        push(
            ctxv.at[:, ctx_cols(flip(chip, k // 2))], ctxg.at[k // 2],
            ctx_s.at[k // 2], ctx_r.at[k // 2], to_seq(k),
        )
    own_kw.wait()
    own_vw.wait()
    push(kvw.at[core], kvw.at[core], w_s, w_r, to_seq(1))
    for k in list(masks) + [k + 1 for k in masks] + [1]:
        push(ow.at[ow_piece(flip(s, k)), :], spread.at[s], sp_s.at[k], sp_r.at[k], to_seq(k))
    own_qw.wait()
    half_slot = half_rows
    gather_own(half_slot, 0, chip_bits[:1], qw_s, qw_r)
    gather_own(half_slot, 1, chip_bits[1:], qw_s, qw_r)
    gather_core(half_slot, 0, qw_s, qw_r)
    gather_core(half_slot, 1, qw_s, qw_r)

    own_vid.wait()
    strip = 16

    with jax.named_scope("norm"):
        @pl.loop(0, tok // strip)
        def _(i):
            at = pl.ds(pl.multiple_of(i * strip, strip), strip)
            rows = vid[at, :].astype(F32)
            mean = jnp.mean(rows, axis=-1, keepdims=True)
            centred = rows - mean
            spread_ = jnp.mean(centred * centred, axis=-1, keepdims=True)
            normed[at, :] = (centred * (1.0 / jnp.sqrt(spread_ + 1e-06))).astype(BF16)

    with jax.named_scope("kv"):
        arrived(kvw.at[1 - core], w_s, w_r, to_seq(1))

        def partial_kv(source):
            return jnp.dot(source, kvw[...].reshape(pair, 2 * att), preferred_element_type=F32)

        mine = partial_kv(ctxv[:, ctx_cols(chip)])
        for k in masks:
            c = k // 2
            arrived(ctxg.at[c], ctx_s.at[c], ctx_r.at[c], to_seq(k))
            block = partial_kv(ctxg[c])
            cks[c] = block[:, :att]
            cvs[c] = block[:, att:].astype(BF16)
            push(cks.at[c], ckr.at[c], ck_s.at[c], ck_r.at[c], to_seq(k))
            push(cvs.at[c], cvr.at[c], cv_s.at[c], cv_r.at[c], to_seq(k))
        cks[0] = mine[:, :att]
        ckr[0] = mine[:, att:]
    gather_own(half_slot, 0, chip_bits[1:], qw_s, qw_r)
    gather_own(half_slot, 1, chip_bits[:1], qw_s, qw_r)

    def chip_queries(p):
        lanes = pl.ds(pl.multiple_of(p * pair, pair), pair)
        return jnp.dot(normed[:, lanes], qwg[lanes, :], preferred_element_type=F32)

    with jax.named_scope("shsc"):
        own_tw.wait()
        for i in range(2):
            shsc[i] = mod[i : i + 1, :] + jnp.dot(act[...], tw[i], preferred_element_type=F32)[:8]

    with jax.named_scope("relay1"):
        first = [(0, b) for b in chip_bits[:1]] + [(1, b) for b in chip_bits[1:]]
        for half, b in first:
            gather_relay(half_slot, half, b, qw_s, qw_r)
        for half in range(2):
            gather_end(half_slot, half, 0, qw_s, qw_r)
    with jax.named_scope("q_own"):
        queries[...] = chip_queries(chip)

    def own_cols(zz):
        return pl.ds(zz * ratio, ratio)

    def ow_slot_z(p):
        return owg.at[:, p, ow_piece(s), :]

    with jax.named_scope("spread"):
        own_spread.wait()
        for k in list(masks) + [k + 1 for k in masks] + [1]:
            arrived(spread.at[flip(s, k)], sp_s.at[k], sp_r.at[k], to_seq(k))
        own_ow = load(spread.at[own_cols(z)], ow_slot_z(z), 7)
        for k in range(1, n_head):
            push(
                spread.at[own_cols(flip(z, k))], ow_slot_z(z), oz_s.at[k], oz_r.at[k], to_head(k)
            )

    with jax.named_scope("kv_sum"):
        key_rows = cks[0]
        value_rows = ckr[0]
        for k in masks:
            c = k // 2
            arrived(ckr.at[c], ck_s.at[c], ck_r.at[c], to_seq(k))
            arrived(cvr.at[c], cv_s.at[c], cv_r.at[c], to_seq(k))
            key_rows = key_rows + ckr[c]
            value_rows = value_rows + cvr[c].astype(F32)
        cks[0] = key_rows
        ksq[0] = column_to_row(jnp.sum(key_rows * key_rows, axis=1, keepdims=True))
        for k in range(1, n_head):
            push(ksq.at[0], ksq.at[k], ksq_s.at[k], ksq_r.at[k], to_head(k))
        vall[s] = value_rows.astype(BF16)
        for k in masks + [1]:
            push(vall.at[s], vall.at[s], v_s.at[k], v_r.at[k], to_seq(k))

    with jax.named_scope("relay2"):
        second = [(0, b) for b in chip_bits[1:]] + [(1, b) for b in chip_bits[:1]]
        for half, b in second:
            gather_relay(half_slot, half, b, qw_s, qw_r)

    with jax.named_scope("k_norm"):
        for k in range(1, n_head):
            arrived(ksq.at[k], ksq_s.at[k], ksq_r.at[k], to_head(k))
        k_mean = row_to_column(jnp.sum(ksq[...], axis=0), text) / (att * n_head)
        kall[s] = (cks[0] / jnp.sqrt(k_mean + 1e-06) * kg[...]).astype(BF16)
        for k in masks + [1]:
            push(kall.at[s], kall.at[s], k_s.at[k], k_r.at[k], to_seq(k))

    with jax.named_scope("q_mid"):
        for b in chip_bits:
            for half in range(2):
                gather_end(half_slot, half, b, qw_s, qw_r)
            queries[...] += chip_queries(flip(chip, b // 2))
    with jax.named_scope("q_far"):
        for k in masks:
            if k not in chip_bits:
                for half in range(2):
                    gather_relay(half_slot, half, k, qw_s, qw_r)
        for k in masks:
            if k not in chip_bits:
                for half in range(2):
                    gather_end(half_slot, half, k, qw_s, qw_r)
                queries[...] += chip_queries(flip(chip, k // 2))
        q = queries[...]
        qsq[0] = column_to_row(jnp.sum(q * q, axis=1, keepdims=True))
        for k in range(1, n_head):
            push(qsq.at[0], qsq.at[k], qsq_s.at[k], qsq_r.at[k], to_head(k))

    def ow_half(half, p):
        rows = piece // 2 if ratio == 1 else piece
        if ratio == 1:
            return owg.at[:, :, pl.ds(pl.multiple_of(p * piece + half * rows, rows), rows), :]
        cut = ratio // 2
        return owg.at[pl.ds(half * cut, cut), :, ow_piece(p), :]

    with jax.named_scope("ow_start"):
        own_ow.wait()
        for k in range(1, n_head):
            arrived(ow_slot_z(flip(z, k)), oz_s.at[k], oz_r.at[k], to_head(k))
        gather_own(ow_half, 0, chip_bits[:1], og_s, og_r)
        gather_own(ow_half, 1, chip_bits[1:], og_s, og_r)
        gather_own(ow_half, 0, chip_bits[1:], og_s, og_r)
        gather_own(ow_half, 1, chip_bits[:1], og_s, og_r)
        for half in range(2):
            gather_core(ow_half, half, og_s, og_r)

    with jax.named_scope("kv_in"):
        for ref, ssem, rsem in ((vall, v_s, v_r), (kall, k_s, k_r)):
            for k in masks:
                here = ref.at[flip(s, k)]
                arrived(here, ssem.at[k], rsem.at[k], to_seq(k))
                push(here, here, ssem.at[k + 1], rsem.at[k + 1], to_seq(1))
        for ref, ssem, rsem in ((vall, v_s, v_r), (kall, k_s, k_r)):
            for k in [0] + masks:
                arrived(ref.at[flip(s, k + 1)], ssem.at[k + 1], rsem.at[k + 1], to_seq(1))

    with jax.named_scope("q_norm"):
        for k in range(1, n_head):
            arrived(qsq.at[k], qsq_s.at[k], qsq_r.at[k], to_head(k))
        q_mean = row_to_column(jnp.sum(qsq[...], axis=0), tok) / (att * n_head)
        q_normed = (queries[...] / jnp.sqrt(q_mean + 1e-06) * qg[...]).astype(BF16)

    step = tok // chunks

    def next_head(way):
        return (s, z + way)

    def held(way, d):
        return attg.at[d % n_head if way > 0 else (n_head - d) % n_head]

    def reach(way, origin_ok, c, d):
        at = slice(c * step, (c + 1) * step)
        side = 0 if way > 0 else 1
        ok = origin_ok & ((z + way >= 0) & (z + way < n_head))
        copy = remote(
            held(way, d - 1).at[at], held(way, d).at[at],
            at_s.at[side, c, d], at_r.at[side, c, d], next_head(way),
        )

        @pl.when(ok)
        def _():
            copy.start()

        sent.append((ok, copy))

    def take(way, c, d):
        at = slice(c * step, (c + 1) * step)
        side = 0 if way > 0 else 1
        origin = z - way * d
        ok = (origin >= 0) & (origin < n_head)

        @pl.when(ok)
        def _():
            arrived(held(way, d).at[at], at_s.at[side, c, d], at_r.at[side, c, d], next_head(-way))

        return ok

    all_text = n_seq * text
    with jax.named_scope("attend"):
        every_k = kall[...].reshape(all_text, att)
        every_v = vall[...].reshape(all_text, att)
        seen = lax.broadcasted_iota(jnp.int32, (1, all_text), 1) < valid[0]
        for c in range(chunks):
            at = slice(c * step, (c + 1) * step)
            for h in range(att // HD):
                lanes = slice(h * HD, (h + 1) * HD)
                scores = lax.dot_general(
                    q_normed[at, lanes], every_k[:, lanes], (((1,), (1,)), ((), ())),
                    preferred_element_type=F32,
                ) * HD ** (-0.5)
                scores = jnp.where(seen, scores, F32(-1e30))
                shifted = jnp.exp(scores - jnp.max(scores, axis=-1, keepdims=True))
                weights = (shifted * (1.0 / jnp.sum(shifted, axis=-1, keepdims=True))).astype(BF16)
                attg[0, at, lanes] = jnp.dot(
                    weights, every_v[:, lanes], preferred_element_type=F32
                ).astype(BF16)
            for way in (1, -1):
                reach(way, z >= 0, c, 1)

    def ow_relays(pairs):
        for half, b in pairs:
            gather_relay(ow_half, half, b, og_s, og_r)

    for d in range(1, n_head - 1):
        for c in range(chunks):
            with jax.named_scope(f"pass{d}_{c}"):
                for way in (1, -1):
                    ok = take(way, c, d)
                    reach(way, ok, c, d + 1)
            if d == 1 and c == 0:
                with jax.named_scope("ow1"):
                    ow_relays(first)
            if d == 1 and c == chunks - 1:
                with jax.named_scope("ow2"):
                    ow_relays(second)
    with jax.named_scope("ow3"):
        for k in masks:
            if k not in chip_bits:
                for half in range(2):
                    gather_relay(ow_half, half, k, og_s, og_r)
        for k in [0] + masks:
            for half in range(2):
                gather_end(ow_half, half, k, og_s, og_r)

    cols = owg.shape[3]
    part_width = mod_out.shape[1]
    for c in range(chunks):
        at = slice(c * step, (c + 1) * step)
        with jax.named_scope(f"last{c}"):
            for way in (1, -1):
                take(way, c, n_head - 1)
        with jax.named_scope(f"project{c}"):
            row_sum = jnp.zeros((step, 1), F32)
            row_sq = jnp.zeros((step, 1), F32)
            for j in range(ratio):
                here = slice(j * cols, (j + 1) * cols)
                projected = jnp.dot(attg[0, at], owg[j, z], preferred_element_type=F32)
                for k in range(1, n_head):
                    projected = projected + jnp.dot(
                        attg[k, at], owg[j, lax.rem(z + n_head - k, n_head)], preferred_element_type=F32
                    )
                if vpart is None:
                    base = vid[at, pl.ds(pl.multiple_of(z * part_width + j * cols, LANES), cols)]
                else:
                    base = vpart[at, here]
                rounded = (base.astype(F32) + projected).astype(BF16)
                resid_out[at, here] = rounded
                wide = rounded.astype(F32)
                row_sum = row_sum + jnp.sum(wide, axis=1, keepdims=True)
                row_sq = row_sq + jnp.sum(wide * wide, axis=1, keepdims=True)
            stat[c, 0, :1] = column_to_row(row_sum)[:, :step]
            stat[c, 0, 1:] = column_to_row(row_sq)[:, :step]
            for k in range(1, n_head):
                push(stat.at[c, 0], stat.at[c, k], st_s.at[c, k], st_r.at[c, k], to_head(k))
    for c in range(chunks):
        at = slice(c * step, (c + 1) * step)
        with jax.named_scope(f"stat{c}"):
            for k in range(1, n_head):
                arrived(stat.at[c, k], st_s.at[c, k], st_r.at[c, k], to_head(k))
        with jax.named_scope(f"modulate{c}"):
            both = jnp.sum(stat[c], axis=0) / (part_width * n_head)
            mean2 = both[:1]
            inverse = 1.0 / jnp.sqrt(both[1:] - mean2 * mean2 + 1e-06)
            mean_col = row_to_column(mean2, step)
            inv_col = row_to_column(inverse, step)
            wide = resid_out[at, :].astype(F32)
            mod_out[at, :] = (
                (wide - mean_col) * inv_col * (1.0 + shsc[1, :1, :]) + shsc[0, :1, :]
            ).astype(BF16)
    for ok, copy in sent:
        if ok is None:
            copy.wait_send()
        else:
            pl.when(ok)(copy.wait_send)


def on_device(
    n_seq,
    n_head,
    video_rows,
    context,
    valid_length,
    timestep,
    query_weight,
    key_weight,
    value_weight,
    out_weight,
    query_gain,
    key_gain,
    time_weight,
    modulation,
):
    tok, width = video_rows.shape
    text = context.shape[0]
    depth, att = query_weight.shape
    cols = out_weight.shape[1]
    part_width = modulation.shape[1]
    ratio = n_seq // n_head
    n_chip = n_seq // 2
    chunks = 4
    piece = out_weight.shape[0] // n_seq
    half = FREQ // 2
    freqs = jnp.exp(-jnp.log(10000.0) * jnp.arange(half, dtype=F32) / half)
    angles = timestep[0].astype(F32) * freqs
    embedding = jnp.concatenate([jnp.cos(angles), jnp.sin(angles)])
    act = jnp.broadcast_to(jax.nn.silu(embedding).astype(BF16)[None, :], (16, FREQ))
    sliced = part_width % LANES != 0 or cols % LANES != 0
    extra = []
    if sliced:
        extra.append(
            lax.dynamic_slice_in_dim(
                video_rows, lax.axis_index("head") * part_width, part_width, 1
            )
        )
    vmem = pl.BlockSpec(memory_space=pltpu.VMEM)
    hbm = pl.BlockSpec(memory_space=pl.ANY)
    dma = pltpu.SemaphoreType.DMA
    return pl.pallas_call(
        functools.partial(body, n_seq, n_head, chunks, sliced),
        out_shape=[jax.ShapeDtypeStruct((tok, part_width), BF16)] * 2,
        in_specs=[pl.BlockSpec(memory_space=pltpu.SMEM)]
        + [hbm] * 6
        + [vmem] * 3
        + [hbm, vmem]
        + [vmem] * len(extra),
        out_specs=[vmem] * 2,
        scratch_shapes=[
            pltpu.VMEM((tok, width), BF16),
            pltpu.VMEM((tok, width), BF16),
            pltpu.VMEM((text, width), BF16),
            pltpu.VMEM((n_chip, text, 2 * depth), BF16),
            pltpu.VMEM((n_seq * depth, att), BF16),
            pltpu.VMEM((2, depth, 2 * att), BF16),
            pltpu.VMEM((n_chip, text, att), F32),
            pltpu.VMEM((n_chip, text, att), F32),
            pltpu.VMEM((n_chip, text, att), BF16),
            pltpu.VMEM((n_chip, text, att), BF16),
            pltpu.VMEM((n_seq, text, att), BF16),
            pltpu.VMEM((n_seq, text, att), BF16),
            pltpu.VMEM((n_seq, piece, cols), BF16),
            pltpu.VMEM((ratio, n_head, out_weight.shape[0], cols), BF16),
            pltpu.VMEM((n_head, tok, att), BF16),
            pltpu.VMEM((tok, att), F32),
            pltpu.VMEM((n_head, 1, tok), F32),
            pltpu.VMEM((n_head, 1, -(-text // LANES) * LANES), F32),
            pltpu.VMEM((chunks, n_head, 2, tok // chunks), F32),
            pltpu.VMEM((2, 8, part_width), F32),
            pltpu.VMEM(time_weight.shape, BF16),
            dma((8,)),
            *[dma((n_chip,))] * 2,
            *[dma((2, n_seq))] * 2,
            *[dma] * 2,
            *[dma((n_chip,))] * 2,
            *[dma((n_chip,))] * 2,
            *[dma((n_seq,))] * 2,
            *[dma((n_seq,))] * 2,
            *[dma((n_seq,))] * 2,
            *[dma((n_head,))] * 2,
            *[dma((2, n_seq))] * 2,
            *[dma((n_head,))] * 2,
            *[dma((n_head,))] * 2,
            *[dma((2, chunks, n_head))] * 2,
            *[dma((chunks, n_head))] * 2,
        ],
        compiler_params=pltpu.CompilerParams(
            collective_id=0, has_side_effects=True, vmem_limit_bytes=60 * 1024 * 1024
        ),
    )(
        valid_length,
        video_rows,
        context,
        query_weight,
        key_weight,
        value_weight,
        out_weight,
        query_gain[None, :],
        key_gain[None, :],
        act,
        time_weight,
        modulation,
        *extra,
    )


def solution(mesh):
    in_specs = (
        P("seq", None),
        P("seq", None),
        P(),
        P(),
        P("seq", "head"),
        P("seq", "head"),
        P("seq", "head"),
        P("head", "seq"),
        P("head"),
        P("head"),
        P(None, None, "head"),
        P(None, "head"),
    )
    out_specs = (P("seq", "head"), P("seq", "head"))
    return jax.shard_map(
        functools.partial(on_device, mesh.shape["seq"], mesh.shape["head"]),
        mesh=mesh, in_specs=in_specs, out_specs=out_specs, check_vma=False,
    )
```

time: 97.9 us -> 74.2 us (0.76)
  Pallas kernels: 91.4 us -> 67.7 us
    pallas_call x1, Pallas kernels: 91.4 us -> 67.7 us  [on_device(): pl.pallas_call(functools.partial(body, n_seq, n_head, chunks, sliced), ou...]
where the time goes in v1:
time: 74.2 us; the launch traced here: 74 us
  Pallas kernels  67.7 us (91%)
  local copies, waits for them, and re-layouts  4.24 us (6%)
  between operations  1.95 us (3%)
    pallas_call x1, Pallas kernels, on_device(): pl.pallas_call(functools.partial(body, n_seq, n_head, chunks, sliced), ou...  67.7 us
    unnamed x4, local copies, waits for them, and re-layouts  3.62 us

profile of v1, /device:TPU:0, one launch (start us, length us, event | category | flops | bytes accessed | tf_op | source)
XLA Modules:
  0.0 74.0 jit_solution(47303451439083861)
XLA Ops:
  2.0 0.6 broadcast_in_dim.14.refs_9_
  2.6 67.7 %shard_map.131 = (bf16[512,1280]{1,0:T(8,128)(2,1)}, bf16[512,1280]{1,0:T(8,128)(2,1)}) custom-call(s32[1]{0:T(128)S(6)} %copy.16.refs_0_, bf16[512,5120]{1,0:T(8,128)(2,1)} %refs_1_.1, bf16[64,5120]{1,0:T(8,128)(2,1)} %refs_2_.1, bf16[640,256]{1,0:T(8,128)(2,1)} %refs_3_.1, bf16[640,256]{1,0:T(8,128)(2,1)} %refs_4_.1, bf16[640,256]{1,0:T(8,128)(2,1)} %refs_5_.1, ...), custom_call_target="tpu_custom_call" | custom-call | tf_op jit(solution)/shard_map/pallas_call | solution.py:497
  70.3 0.0 copy-start
  70.3 2.6 %copy.18 = bf16[512,1280]{1,0:T(8,128)(2,1)} copy(bf16[512,1280]{1,0:T(8,128)(2,1)} %get-tuple-element.6) | data formatting | bytes 2621440
  72.9 0.0 copy-done
  72.9 1.1 %copy.19 = bf16[512,1280]{1,0:T(8,128)(2,1)} copy(bf16[512,1280]{1,0:T(8,128)(2,1)S(1)} %copy-done) | data formatting | bytes 2621440
  (2 shorter events, 0.1 us)
Async XLA Ops:
  70.3 2.6 %copy-start = (bf16[512,1280]{1,0:T(8,128)(2,1)S(1)}, bf16[512,1280]{1,0:T(8,128)(2,1)}, u32[]{:S(2)}) copy-start(bf16[512,1280]{1,0:T(8,128)(2,1)} %get-tuple-element.7) | copy-start | bytes 3932164

commit v2 on v1

v2 whole, which is shorter than its diff:
```python
import functools

import jax
import jax.numpy as jnp
import numpy as np
from jax import lax
from jax.experimental import pallas as pl
from jax.experimental.pallas import tpu as pltpu
from jax.sharding import PartitionSpec as P

HD = 128
FREQ = 256
LANES = 128
VMEM_MOST = 67_000_000
NORM_FIRST = 9
F32 = jnp.float32
BF16 = jnp.bfloat16
MESH_ID = pl.DeviceIdType.MESH


def flip(index, mask):
    bit = 1
    while bit <= mask:
        if mask & bit:
            index = index + bit - 2 * bit * ((index // bit) % 2)
        bit *= 2
    return index


def bits_of(mask):
    return [1 << b for b in range(mask.bit_length()) if mask >> b & 1]


def last_bit(half, mask):
    return bits_of(mask)[-1] if half == 0 else bits_of(mask)[0]


def by_hops(n_seq):
    return sorted(range(2, n_seq, 2), key=lambda k: (len(bits_of(k)), k))


def column_to_row(column):
    tall = column.shape[0]
    wide = -(-tall // LANES) * LANES
    if wide > tall:
        column = jnp.concatenate([column, jnp.zeros((wide - tall, 1), F32)], axis=0)
    return jnp.transpose(jnp.broadcast_to(column, (wide, LANES)))[:1]


def row_to_column(row, tall):
    return jnp.transpose(jnp.broadcast_to(row, (LANES, row.shape[1])))[:tall, :1]


def body(n_seq, n_head, cuts, sliced, *refs):
    if sliced:
        steps(n_seq, n_head, cuts, *refs)
    else:
        steps(n_seq, n_head, cuts, *refs[:13], None, *refs[13:])


def steps(
    n_seq, n_head, cuts,
    valid, when, video, ctx, qw, kw, vw, ow, qg_hbm, kg_hbm, freqs_hbm, tw_hbm, mod_hbm, vpart,
    resid_out, mod_out,
    vid, normed, ctxv, ctxg, qwg, kvw, cks, ckr, cvs, cvr, kall, vall, spread, owg, attg,
    queries, qsq, ksq, stat, shsc, tw, qg, kg, freqs, mod,
    loc_sem, send_sem, pass_s, ctx_r, ctz_r, qw_r, qc_r, og_r, oc_r, at_r, st_r, one_r,
):
    s = lax.axis_index("seq")
    z = lax.axis_index("head")
    core = s % 2
    chip = s // 2
    n_chip = n_seq // 2
    ratio = n_seq // n_head
    chunks = len(cuts)
    tok, width = vid.shape
    depth = qw.shape[0]
    att = qw.shape[1]
    text = ctx.shape[0]
    pair = 2 * depth
    masks = by_hops(n_seq)
    chip_bits = [k for k in masks if len(bits_of(k)) == 1]
    far = [k for k in masks if k not in chip_bits]
    (S_CTX, S_CTZ, S_W, S_SP, S_QW, S_CK, S_CV, S_KSQ, S_QSQ, S_V, S_K, S_OZ, S_OG, S_ST) = range(14)
    (R_W, R_SP, R_CK, R_CV, R_KSQ, R_QSQ, R_V, R_VC, R_K, R_KC, R_OZ) = range(11)

    def to_seq(k):
        return (flip(s, k), z)

    def to_head(k):
        return (s, flip(z, k))

    def remote(src, dst, ssem, rsem, dev):
        return pltpu.make_async_remote_copy(
            src_ref=src, dst_ref=dst, send_sem=ssem, recv_sem=rsem,
            device_id=dev, device_id_type=MESH_ID,
        )

    def push(src, dst, group, rsem, dev):
        remote(src, dst, send_sem.at[group], rsem, dev).start()

    def arrived(ref, sem):
        remote(ref, ref, sem, sem, to_seq(1)).wait_recv()

    def left(ref, sem):
        remote(ref, ref, sem, sem, to_seq(1)).wait_send()

    def gather_own(slot, half, bits, group, rsem):
        for b in bits:
            push(slot(half, s), slot(half, s), group, rsem.at[half, b // 2], to_seq(b))

    def gather_core(slot, group, csem):
        for half in range(2):
            push(slot(half, s), slot(half, s), group, csem.at[0], to_seq(1))

    def gather_relay(slot, half, k, group, rsem, csem):
        here = slot(half, flip(s, k))
        arrived(here, rsem.at[half, k // 2])
        for b in chip_bits:
            if not k & b and last_bit(half, k | b) == b:
                push(here, here, group, rsem.at[half, (k | b) // 2], to_seq(b))
        push(here, here, group, csem.at[k // 2], to_seq(1))

    barrier = pltpu.get_barrier_semaphore()
    for k in range(1, n_seq):
        pl.semaphore_signal(barrier, inc=1, device_id=to_seq(k), device_id_type=MESH_ID)
    for k in range(1, n_head):
        pl.semaphore_signal(barrier, inc=1, device_id=to_head(k), device_id_type=MESH_ID)

    def shard_rows(p, count=1):
        return qwg.at[pl.ds(pl.multiple_of(p * depth, depth), count * depth), :]

    def half_rows(half, p):
        rows = depth // 2
        return qwg.at[pl.ds(pl.multiple_of(p * depth + half * rows, rows), rows), :]

    def load(src, dst, i):
        copy = pltpu.make_async_copy(src, dst, loc_sem.at[i])
        copy.start()
        return copy

    piece = ow.shape[0] // n_seq

    def ow_piece(p):
        return pl.ds(pl.multiple_of(p * piece, piece), piece)

    own_ctx = load(ctx, ctxv, 0)
    own_qw = load(qw, shard_rows(s), 1)
    own_kw = load(kw, kvw.at[core, :, :att], 2)
    own_vw = load(vw, kvw.at[core, :, att:], 3)
    own_vid = load(video, vid, 4)
    own_spread = load(ow.at[ow_piece(s), :], spread.at[s], 5)
    own_tw = load(tw_hbm, tw, 6)
    small = [
        load(a, b, 8 + i)
        for i, (a, b) in enumerate(((qg_hbm, qg), (kg_hbm, kg), (freqs_hbm, freqs), (mod_hbm, mod)))
    ]
    with jax.named_scope("barrier"):
        pl.semaphore_wait(barrier, n_seq + n_head - 2)

    def ctx_cols(p):
        return pl.ds(pl.multiple_of(p * pair, pair), pair)

    part = text // 2

    def ctx_rows(q):
        return pl.ds(pl.multiple_of(q * part, part), part)

    mine = z % 2
    own_ctx.wait()
    for k in far + chip_bits:
        push(
            ctxv.at[ctx_rows(mine), ctx_cols(flip(chip, k // 2))], ctxg.at[k // 2, ctx_rows(mine)],
            S_CTX, ctx_r.at[k // 2], to_seq(k),
        )
    own_kw.wait()
    own_vw.wait()
    push(kvw.at[core], kvw.at[core], S_W, one_r.at[R_W], to_seq(1))
    for k in masks + [k + 1 for k in masks] + [1]:
        push(ow.at[ow_piece(flip(s, k)), :], spread.at[s], S_SP, one_r.at[R_SP], to_seq(k))
    own_qw.wait()
    first = [(0, b) for b in chip_bits[:1]] + [(1, b) for b in chip_bits[1:]]
    second = [(0, b) for b in chip_bits[1:]] + [(1, b) for b in chip_bits[:1]]
    for half, b in first + second:
        gather_own(half_rows, half, [b], S_QW, qw_r)
    gather_core(half_rows, S_QW, qc_r)

    own_vid.wait()
    strip = 16
    strips = tok // strip

    def norm(begin, end):
        with jax.named_scope("norm"):
            @pl.loop(begin, end)
            def _(i):
                at = pl.ds(pl.multiple_of(i * strip, strip), strip)
                rows = vid[at, :].astype(F32)
                mean = jnp.mean(rows, axis=-1, keepdims=True)
                centred = rows - mean
                spread_ = jnp.mean(centred * centred, axis=-1, keepdims=True)
                normed[at, :] = (centred * (1.0 / jnp.sqrt(spread_ + 1e-06))).astype(BF16)

    norm(0, strips * NORM_FIRST // 16)
    with jax.named_scope("ctx_share"):
        for k in far + chip_bits:
            here = ctxg.at[k // 2, ctx_rows(mine)]
            arrived(here, ctx_r.at[k // 2])
            push(here, here, S_CTZ, ctz_r.at[k // 2], to_head(1))
    norm(strips * NORM_FIRST // 16, strips)

    with jax.named_scope("kv"):
        arrived(kvw.at[1 - core], one_r.at[R_W])

        def partial_kv(source):
            return jnp.dot(source, kvw[...].reshape(pair, 2 * att), preferred_element_type=F32)

        block = partial_kv(ctxv[:, ctx_cols(chip)])
        cks[0] = block[:, :att]
        ckr[0] = block[:, att:]
        for k in far + chip_bits:
            c = k // 2
            arrived(ctxg.at[c, ctx_rows(1 - mine)], ctz_r.at[c])
            block = partial_kv(ctxg[c])
            cks[c] = block[:, :att]
            cvs[c] = block[:, att:].astype(BF16)
            push(cks.at[c], ckr.at[c], S_CK, one_r.at[R_CK], to_seq(k))
            push(cvs.at[c], cvr.at[c], S_CV, one_r.at[R_CV], to_seq(k))

    def chip_queries(p):
        lanes = pl.ds(pl.multiple_of(p * pair, pair), pair)
        return jnp.dot(normed[:, lanes], qwg[lanes, :], preferred_element_type=F32)

    with jax.named_scope("relay1"):
        for half, b in first:
            gather_relay(half_rows, half, b, S_QW, qw_r, qc_r)

    def own_cols(zz):
        return pl.ds(zz * ratio, ratio)

    def ow_slot_z(p):
        return owg.at[:, p, ow_piece(s), :]

    with jax.named_scope("spread"):
        own_spread.wait()
        arrived(spread.at[pl.ds(0, n_seq - 1)], one_r.at[R_SP])
        own_ow = load(spread.at[own_cols(z)], ow_slot_z(z), 7)
        for k in range(1, n_head):
            push(spread.at[own_cols(flip(z, k))], ow_slot_z(z), S_OZ, one_r.at[R_OZ], to_head(k))

    with jax.named_scope("relay2"):
        for half, b in second:
            gather_relay(half_rows, half, b, S_QW, qw_r, qc_r)
        arrived(shard_rows(flip(s, 1)), qc_r.at[0])
    with jax.named_scope("q_own"):
        queries[...] = chip_queries(chip)
    with jax.named_scope("shsc"):
        own_tw.wait()
        for copy in small:
            copy.wait()
        angles = jnp.broadcast_to(when[0].astype(F32) * freqs[...], (16, freqs.shape[1]))
        embedding = jnp.concatenate([jnp.cos(angles), jnp.sin(angles)], axis=1)
        act = (embedding / (1.0 + jnp.exp(-embedding))).astype(BF16)
        for i in range(2):
            shsc[i] = mod[i : i + 1, :] + jnp.dot(act, tw[i], preferred_element_type=F32)[:8]

    with jax.named_scope("kv_sum"):
        arrived(ckr.at[pl.ds(1, n_chip - 1)], one_r.at[R_CK])
        arrived(cvr.at[pl.ds(1, n_chip - 1)], one_r.at[R_CV])
        key_rows = cks[0]
        value_rows = ckr[0]
        for c in range(1, n_chip):
            key_rows = key_rows + ckr[c]
            value_rows = value_rows + cvr[c].astype(F32)
        cks[0] = key_rows
        ksq[0] = column_to_row(jnp.sum(key_rows * key_rows, axis=1, keepdims=True))
        for k in range(1, n_head):
            push(ksq.at[0], ksq.at[k], S_KSQ, one_r.at[R_KSQ], to_head(k))
        vall[s] = value_rows.astype(BF16)
        for k in masks:
            push(vall.at[s], vall.at[s], S_V, one_r.at[R_V], to_seq(k))
        push(vall.at[s], vall.at[s], S_V, one_r.at[R_VC], to_seq(1))

    with jax.named_scope("q_mid"):
        for b in chip_bits:
            arrived(shard_rows(flip(s, b + 1)), qc_r.at[b // 2])
            queries[...] += chip_queries(flip(chip, b // 2))

    with jax.named_scope("k_norm"):
        arrived(ksq.at[pl.ds(1, n_head - 1)], one_r.at[R_KSQ])
        k_mean = row_to_column(jnp.sum(ksq[...], axis=0), text) / (att * n_head)
        kall[s] = (cks[0] / jnp.sqrt(k_mean + 1e-06) * kg[...]).astype(BF16)
        for k in masks:
            push(kall.at[s], kall.at[s], S_K, one_r.at[R_K], to_seq(k))
        push(kall.at[s], kall.at[s], S_K, one_r.at[R_KC], to_seq(1))

    with jax.named_scope("q_far"):
        for k in far:
            for half in range(2):
                gather_relay(half_rows, half, k, S_QW, qw_r, qc_r)
        for k in far:
            arrived(shard_rows(flip(s, k + 1)), qc_r.at[k // 2])
            queries[...] += chip_queries(flip(chip, k // 2))
        q = queries[...]
        qsq[0] = column_to_row(jnp.sum(q * q, axis=1, keepdims=True))
        for k in range(1, n_head):
            push(qsq.at[0], qsq.at[k], S_QSQ, one_r.at[R_QSQ], to_head(k))

    def ow_half(half, p):
        if ratio == 1:
            rows = piece // 2
            return owg.at[:, :, pl.ds(pl.multiple_of(p * piece + half * rows, rows), rows), :]
        cut = ratio // 2
        return owg.at[pl.ds(half * cut, cut), :, ow_piece(p), :]

    def ow_slot(p):
        return owg.at[:, :, ow_piece(p), :]

    with jax.named_scope("ow_start"):
        own_ow.wait()
        arrived(owg.at[:, pl.ds(0, n_head - 1), ow_piece(s), :], one_r.at[R_OZ])
        for half, b in first + second:
            gather_own(ow_half, half, [b], S_OG, og_r)
        gather_core(ow_half, S_OG, oc_r)

    with jax.named_scope("kv_in"):
        for ref, group, chips in ((vall, S_V, R_V), (kall, S_K, R_K)):
            arrived(ref.at[pl.ds(0, n_chip - 1)], one_r.at[chips])
            for k in masks:
                here = ref.at[flip(s, k)]
                push(here, here, group, one_r.at[chips + 1], to_seq(1))
        for ref, chips in ((vall, R_V), (kall, R_K)):
            arrived(ref.at[pl.ds(0, n_chip)], one_r.at[chips + 1])

    with jax.named_scope("q_norm"):
        arrived(qsq.at[pl.ds(1, n_head - 1)], one_r.at[R_QSQ])
        q_mean = row_to_column(jnp.sum(qsq[...], axis=0), tok) / (att * n_head)
        q_normed = (queries[...] / jnp.sqrt(q_mean + 1e-06) * qg[...]).astype(BF16)

    def held(way, d):
        return d % n_head if way > 0 else (n_head - d) % n_head

    def onward(way, d):
        origin = z - way * (d - 1)
        return (origin >= 0) & (origin < n_head) & (z + way >= 0) & (z + way < n_head)

    def passed(way, d):
        return pass_s.at[0 if way > 0 else 1, d - 1]

    def reach(way, c, d):
        slot = held(way, d)

        @pl.when(onward(way, d))
        def _():
            remote(
                attg.at[held(way, d - 1), cuts[c]], attg.at[slot, cuts[c]],
                passed(way, d), at_r.at[c, slot - 1], (s, z + way),
            ).start()

    def take(way, c, d):
        slot = held(way, d)
        origin = z - way * d

        @pl.when((origin >= 0) & (origin < n_head))
        def _():
            arrived(attg.at[slot, cuts[c]], at_r.at[c, slot - 1])

    all_text = n_seq * text
    with jax.named_scope("attend"):
        every_k = kall[...].reshape(all_text, att)
        every_v = vall[...].reshape(all_text, att)
        seen = lax.broadcasted_iota(jnp.int32, (1, all_text), 1) < valid[0]
        for c in range(chunks):
            at = cuts[c]
            for h in range(att // HD):
                lanes = slice(h * HD, (h + 1) * HD)
                scores = lax.dot_general(
                    q_normed[at, lanes], every_k[:, lanes], (((1,), (1,)), ((), ())),
                    preferred_element_type=F32,
                ) * HD ** (-0.5)
                scores = jnp.where(seen, scores, F32(-1e30))
                shifted = jnp.exp(scores - jnp.max(scores, axis=-1, keepdims=True))
                weights = (shifted * (1.0 / jnp.sum(shifted, axis=-1, keepdims=True))).astype(BF16)
                attg[0, at, lanes] = jnp.dot(
                    weights, every_v[:, lanes], preferred_element_type=F32
                ).astype(BF16)
            for way in (1, -1):
                reach(way, c, 1)

    def ow_relays(pairs):
        for half, b in pairs:
            gather_relay(ow_half, half, b, S_OG, og_r, oc_r)

    for d in range(1, n_head - 1):
        for c in range(chunks):
            with jax.named_scope(f"pass{d}_{c}"):
                for way in (1, -1):
                    take(way, c, d)
                    reach(way, c, d + 1)
            if d == 1 and c == 0:
                with jax.named_scope("ow1"):
                    ow_relays(first)
            if d == 1 and c == chunks - 1:
                with jax.named_scope("ow2"):
                    ow_relays(second)
    with jax.named_scope("left1"):
        few = pl.ds(0, n_chip - 1)
        left(ctxg.at[few, ctx_rows(0)], send_sem.at[S_CTX])
        left(ctxg.at[few, ctx_rows(0)], send_sem.at[S_CTZ])
        left(kvw.at[0], send_sem.at[S_W])
        left(spread.at[pl.ds(0, n_seq - 1)], send_sem.at[S_SP])
        left(shard_rows(0, n_seq - 1), send_sem.at[S_QW])
        left(ckr.at[few], send_sem.at[S_CK])
        left(cvr.at[few], send_sem.at[S_CV])
        left(ksq.at[pl.ds(0, n_head - 1)], send_sem.at[S_KSQ])
        left(qsq.at[pl.ds(0, n_head - 1)], send_sem.at[S_QSQ])
        left(vall.at[pl.ds(0, n_seq - 1)], send_sem.at[S_V])
        left(kall.at[pl.ds(0, n_seq - 1)], send_sem.at[S_K])
        left(owg.at[:, pl.ds(0, n_head - 1), ow_piece(0), :], send_sem.at[S_OZ])
    with jax.named_scope("ow3"):
        for k in far:
            for half in range(2):
                gather_relay(ow_half, half, k, S_OG, og_r, oc_r)
        for k in [0] + masks:
            arrived(ow_slot(flip(s, k + 1)), oc_r.at[k // 2])

    cols = owg.shape[3]
    part_width = mod_out.shape[1]

    def modulate(c):
        at = cuts[c]
        step = at.stop - at.start
        with jax.named_scope(f"stat{c}"):
            arrived(stat.at[c, pl.ds(1, n_head - 1)], st_r.at[c])
        with jax.named_scope(f"modulate{c}"):
            both = jnp.sum(stat[c], axis=0) / (part_width * n_head)
            mean2 = both[:1]
            inverse = 1.0 / jnp.sqrt(both[1:] - mean2 * mean2 + 1e-06)
            mean_col = row_to_column(mean2, step)
            inv_col = row_to_column(inverse, step)
            wide = resid_out[at, :].astype(F32)
            mod_out[at, :] = (
                (wide - mean_col) * inv_col * (1.0 + shsc[1, :1, :]) + shsc[0, :1, :]
            ).astype(BF16)

    for c in range(chunks):
        at = cuts[c]
        step = at.stop - at.start
        with jax.named_scope(f"last{c}"):
            for way in (1, -1):
                take(way, c, n_head - 1)
        with jax.named_scope(f"project{c}"):
            row_sum = jnp.zeros((step, 1), F32)
            row_sq = jnp.zeros((step, 1), F32)
            for j in range(ratio):
                here = slice(j * cols, (j + 1) * cols)
                projected = jnp.dot(attg[0, at], owg[j, z], preferred_element_type=F32)
                for k in range(1, n_head):
                    projected = projected + jnp.dot(
                        attg[k, at], owg[j, lax.rem(z + n_head - k, n_head)],
                        preferred_element_type=F32,
                    )
                if vpart is None:
                    base = vid[at, pl.ds(pl.multiple_of(z * part_width + j * cols, LANES), cols)]
                else:
                    base = vpart[at, here]
                rounded = (base.astype(F32) + projected).astype(BF16)
                resid_out[at, here] = rounded
                wide = rounded.astype(F32)
                row_sum = row_sum + jnp.sum(wide, axis=1, keepdims=True)
                row_sq = row_sq + jnp.sum(wide * wide, axis=1, keepdims=True)
            stat[c, 0, :1] = column_to_row(row_sum)
            stat[c, 0, 1:] = column_to_row(row_sq)
            for k in range(1, n_head):
                push(stat.at[c, 0], stat.at[c, k], S_ST, st_r.at[c], to_head(k))
        if c >= 3:
            modulate(c - 3)
    with jax.named_scope("left2"):
        left(owg.at[:, :, pl.ds(0, piece * (n_seq - 1)), :], send_sem.at[S_OG])
        for way in (1, -1):
            for d in range(1, n_head):
                @pl.when(onward(way, d))
                def _():
                    left(attg.at[0], passed(way, d))
    for c in range(max(chunks - 3, 0), chunks):
        modulate(c)
    left(stat.at[:, pl.ds(0, n_head - 1)], send_sem.at[S_ST])


def put_out(resid, mod, resid_hbm, mod_hbm, sems):
    first = pltpu.make_async_copy(resid, resid_hbm, sems.at[0])
    second = pltpu.make_async_copy(mod, mod_hbm, sems.at[1])
    first.start()
    second.start()
    first.wait()
    second.wait()


def on_device(
    n_seq,
    n_head,
    video_rows,
    context,
    valid_length,
    timestep,
    query_weight,
    key_weight,
    value_weight,
    out_weight,
    query_gain,
    key_gain,
    time_weight,
    modulation,
):
    tok, width = video_rows.shape
    text = context.shape[0]
    depth, att = query_weight.shape
    cols = out_weight.shape[1]
    part_width = modulation.shape[1]
    ratio = n_seq // n_head
    n_chip = n_seq // 2
    quarter = tok // 4
    sizes = [quarter] * 3 + [quarter // 2] * 2
    cuts = [slice(sum(sizes[:c]), sum(sizes[: c + 1])) for c in range(len(sizes))]
    chunks = len(cuts)
    piece = out_weight.shape[0] // n_seq
    half = FREQ // 2
    freqs = np.exp(-np.log(10000.0) * np.arange(half) / half).astype(np.float32)[None, :]
    sliced = part_width % LANES != 0 or cols % LANES != 0
    extra = []
    if sliced:
        extra.append(
            lax.dynamic_slice_in_dim(
                video_rows, lax.axis_index("head") * part_width, part_width, 1
            )
        )
    out_bytes = tok * -(-part_width // LANES) * LANES * 2
    vmem = pl.BlockSpec(memory_space=pltpu.VMEM)
    hbm = pl.BlockSpec(memory_space=pltpu.HBM)
    dma = pltpu.SemaphoreType.DMA
    results = pl.pallas_call(
        functools.partial(body, n_seq, n_head, cuts, sliced),
        out_shape=[pltpu.VMEM((tok, part_width), BF16)] * 2,
        in_specs=[pl.BlockSpec(memory_space=pltpu.SMEM)] * 2
        + [hbm] * 11
        + [vmem] * len(extra),
        out_specs=[vmem] * 2,
        scratch_shapes=[
            pltpu.VMEM((tok, width), BF16),
            pltpu.VMEM((tok, width), BF16),
            pltpu.VMEM((text, width), BF16),
            pltpu.VMEM((n_chip, text, 2 * depth), BF16),
            pltpu.VMEM((n_seq * depth, att), BF16),
            pltpu.VMEM((2, depth, 2 * att), BF16),
            pltpu.VMEM((n_chip, text, att), F32),
            pltpu.VMEM((n_chip, text, att), F32),
            pltpu.VMEM((n_chip, text, att), BF16),
            pltpu.VMEM((n_chip, text, att), BF16),
            pltpu.VMEM((n_seq, text, att), BF16),
            pltpu.VMEM((n_seq, text, att), BF16),
            pltpu.VMEM((n_seq, piece, cols), BF16),
            pltpu.VMEM((ratio, n_head, out_weight.shape[0], cols), BF16),
            pltpu.VMEM((n_head, tok, att), BF16),
            pltpu.VMEM((tok, att), F32),
            pltpu.VMEM((n_head, 1, tok), F32),
            pltpu.VMEM((n_head, 1, -(-text // LANES) * LANES), F32),
            pltpu.VMEM((chunks, n_head, 2, LANES), F32),
            pltpu.VMEM((2, 8, part_width), F32),
            pltpu.VMEM(time_weight.shape, BF16),
            pltpu.VMEM((1, att), F32),
            pltpu.VMEM((1, att), F32),
            pltpu.VMEM((1, half), F32),
            pltpu.VMEM(modulation.shape, F32),
            dma((12,)),
            dma((14,)),
            dma((2, n_head - 1)),
            *[dma((n_chip,))] * 2,
            *[dma((2, n_chip)), dma((n_chip,))] * 2,
            dma((chunks, n_head - 1)),
            dma((chunks,)),
            dma((11,)),
        ],
        compiler_params=pltpu.CompilerParams(
            collective_id=0, has_side_effects=True, vmem_limit_bytes=VMEM_MOST - 2 * out_bytes
        ),
    )(
        valid_length,
        timestep,
        video_rows,
        context,
        query_weight,
        key_weight,
        value_weight,
        out_weight,
        query_gain[None, :],
        key_gain[None, :],
        freqs,
        time_weight,
        modulation,
        *extra,
    )
    return pl.pallas_call(
        put_out,
        out_shape=[jax.ShapeDtypeStruct((tok, part_width), BF16)] * 2,
        in_specs=[vmem] * 2,
        out_specs=[hbm] * 2,
        scratch_shapes=[dma((2,))],
        compiler_params=pltpu.CompilerParams(vmem_limit_bytes=4 * 1024 * 1024),
    )(*results)


def solution(mesh):
    in_specs = (
        P("seq", None),
        P("seq", None),
        P(),
        P(),
        P("seq", "head"),
        P("seq", "head"),
        P("seq", "head"),
        P("head", "seq"),
        P("head"),
        P("head"),
        P(None, None, "head"),
        P(None, "head"),
    )
    out_specs = (P("seq", "head"), P("seq", "head"))
    return jax.shard_map(
        functools.partial(on_device, mesh.shape["seq"], mesh.shape["head"]),
        mesh=mesh, in_specs=in_specs, out_specs=out_specs, check_vma=False,
    )
```

time: 74.2 us -> 64.8 us (0.87)
  Pallas kernels: 67.7 us -> 62.7 us
  local copies, waits for them, and re-layouts: 4.24 us -> 0 us
    pallas_call x1 -> x2, Pallas kernels: 67.7 us -> 62.7 us  [the longest x1 61.2 us: on_device(): pl.pallas_call(functools.partial(body, n_seq, n_head, cuts, sliced), out_...]
    unnamed x4 -> x0, local copies, waits for them, and re-layouts: 3.62 us -> none
where the time goes in v2:
time: 64.8 us; the launch traced here: 64.7 us
  Pallas kernels  62.7 us (97%)
  between operations  1.93 us (3%)
    pallas_call x1, Pallas kernels, on_device(): pl.pallas_call(functools.partial(body, n_seq, n_head, cuts, sliced), out_...  61.2 us
    pallas_call x1, Pallas kernels, on_device(): pl.pallas_call(put_out, out_shape=[jax.ShapeDtypeStruct((tok, part_width)...  1.51 us

profile of v2, /device:TPU:0, one launch (start us, length us, event | category | flops | bytes accessed | tf_op | source)
XLA Modules:
  0.0 64.7 jit_solution(16212064219492875169)
XLA Ops:
  1.9 61.2 %shard_map.140 = (bf16[512,1280]{1,0:T(8,128)(2,1)S(1)}, bf16[512,1280]{1,0:T(8,128)(2,1)S(1)}) custom-call(s32[1]{0:T(128)S(6)} %copy.15.refs_0_, s32[1]{0:T(128)S(6)} %copy.16.refs_1_, bf16[512,5120]{1,0:T(8,128)(2,1)} %refs_2_.1, bf16[64,5120]{1,0:T(8,128)(2,1)} %refs_3_.1, bf16[640,256]{1,0:T(8,128)(2,1)} %refs_4_.1, bf16[640,256]{1,0:T(8,128)(2,1)} %refs_5_.1, ...), custom_call_target="tpu_custom_call" | custom-call | tf_op jit(solution)/shard_map/pallas_call | solution.py:540
  63.2 1.5 %shard_map.141 = (bf16[512,1280]{1,0:T(8,128)(2,1)}, bf16[512,1280]{1,0:T(8,128)(2,1)}) custom-call(bf16[512,1280]{1,0:T(8,128)(2,1)S(1)} %get-tuple-element.4.resid, bf16[512,1280]{1,0:T(8,128)(2,1)S(1)} %get-tuple-element.5.mod), custom_call_target="tpu_custom_call" | custom-call | tf_op jit(solution)/shard_map/pallas_call | solution.py:601

commit v3 on v2

--- a/solution.py
+++ b/solution.py
@@ -13,6 +13,7 @@
 LANES = 128
 VMEM_MOST = 67_000_000
 NORM_FIRST = 9
+OW_FIRST = 3
 F32 = jnp.float32
 BF16 = jnp.bfloat16
 MESH_ID = pl.DeviceIdType.MESH
@@ -60,10 +61,10 @@
 
 def steps(
     n_seq, n_head, cuts,
-    valid, when, video, ctx, qw, kw, vw, ow, qg_hbm, kg_hbm, freqs_hbm, tw_hbm, mod_hbm, vpart,
+    valid_hbm, when_hbm, video, ctx, qw, kw, vw, ow, qg_hbm, kg_hbm, freqs_hbm, tw_hbm, mod_hbm, vpart,
     resid_out, mod_out,
     vid, normed, ctxv, ctxg, qwg, kvw, cks, ckr, cvs, cvr, kall, vall, spread, owg, attg,
-    queries, qsq, ksq, stat, shsc, tw, qg, kg, freqs, mod,
+    queries, qsq, ksq, stat, shsc, tw, qg, kg, freqs, mod, acc, valid, when,
     loc_sem, send_sem, pass_s, ctx_r, ctz_r, qw_r, qc_r, og_r, oc_r, at_r, st_r, one_r,
 ):
     s = lax.axis_index("seq")
@@ -153,7 +154,12 @@
     own_tw = load(tw_hbm, tw, 6)
     small = [
         load(a, b, 8 + i)
-        for i, (a, b) in enumerate(((qg_hbm, qg), (kg_hbm, kg), (freqs_hbm, freqs), (mod_hbm, mod)))
+        for i, (a, b) in enumerate(
+            (
+                (qg_hbm, qg), (kg_hbm, kg), (freqs_hbm, freqs), (mod_hbm, mod),
+                (valid_hbm, valid), (when_hbm, when),
+            )
+        )
     ]
     with jax.named_scope("barrier"):
         pl.semaphore_wait(barrier, n_seq + n_head - 2)
@@ -224,6 +230,8 @@
             cks[c] = block[:, :att]
             cvs[c] = block[:, att:].astype(BF16)
             push(cks.at[c], ckr.at[c], S_CK, one_r.at[R_CK], to_seq(k))
+        for k in far + chip_bits:
+            c = k // 2
             push(cvs.at[c], cvr.at[c], S_CV, one_r.at[R_CV], to_seq(k))
 
     def chip_queries(p):
@@ -265,16 +273,17 @@
 
     with jax.named_scope("kv_sum"):
         arrived(ckr.at[pl.ds(1, n_chip - 1)], one_r.at[R_CK])
-        arrived(cvr.at[pl.ds(1, n_chip - 1)], one_r.at[R_CV])
         key_rows = cks[0]
-        value_rows = ckr[0]
         for c in range(1, n_chip):
             key_rows = key_rows + ckr[c]
-            value_rows = value_rows + cvr[c].astype(F32)
         cks[0] = key_rows
         ksq[0] = column_to_row(jnp.sum(key_rows * key_rows, axis=1, keepdims=True))
         for k in range(1, n_head):
             push(ksq.at[0], ksq.at[k], S_KSQ, one_r.at[R_KSQ], to_head(k))
+        arrived(cvr.at[pl.ds(1, n_chip - 1)], one_r.at[R_CV])
+        value_rows = ckr[0]
+        for c in range(1, n_chip):
+            value_rows = value_rows + cvr[c].astype(F32)
         vall[s] = value_rows.astype(BF16)
         for k in masks:
             push(vall.at[s], vall.at[s], S_V, one_r.at[R_V], to_seq(k))
@@ -292,6 +301,23 @@
         for k in masks:
             push(kall.at[s], kall.at[s], S_K, one_r.at[R_K], to_seq(k))
         push(kall.at[s], kall.at[s], S_K, one_r.at[R_KC], to_seq(1))
+
+    def ow_half(half, p):
+        if ratio == 1:
+            rows = piece // 2
+            return owg.at[:, :, pl.ds(pl.multiple_of(p * piece + half * rows, rows), rows), :]
+        cut = ratio // 2
+        return owg.at[pl.ds(half * cut, cut), :, ow_piece(p), :]
+
+    def ow_slot(p):
+        return owg.at[:, :, ow_piece(p), :]
+
+    with jax.named_scope("ow_start"):
+        own_ow.wait()
+        arrived(owg.at[:, pl.ds(0, n_head - 1), ow_piece(s), :], one_r.at[R_OZ])
+        for half, b in first + second:
+            gather_own(ow_half, half, [b], S_OG, og_r)
+        gather_core(ow_half, S_OG, oc_r)
 
     with jax.named_scope("q_far"):
         for k in far:
@@ -305,23 +331,6 @@
         for k in range(1, n_head):
             push(qsq.at[0], qsq.at[k], S_QSQ, one_r.at[R_QSQ], to_head(k))
 
-    def ow_half(half, p):
-        if ratio == 1:
-            rows = piece // 2
-            return owg.at[:, :, pl.ds(pl.multiple_of(p * piece + half * rows, rows), rows), :]
-        cut = ratio // 2
-        return owg.at[pl.ds(half * cut, cut), :, ow_piece(p), :]
-
-    def ow_slot(p):
-        return owg.at[:, :, ow_piece(p), :]
-
-    with jax.named_scope("ow_start"):
-        own_ow.wait()
-        arrived(owg.at[:, pl.ds(0, n_head - 1), ow_piece(s), :], one_r.at[R_OZ])
-        for half, b in first + second:
-            gather_own(ow_half, half, [b], S_OG, og_r)
-        gather_core(ow_half, S_OG, oc_r)
-
     with jax.named_scope("kv_in"):
         for ref, group, chips in ((vall, S_V, R_V), (kall, S_K, R_K)):
             arrived(ref.at[pl.ds(0, n_chip - 1)], one_r.at[chips])
@@ -363,6 +372,10 @@
         @pl.when((origin >= 0) & (origin < n_head))
         def _():
             arrived(attg.at[slot, cuts[c]], at_r.at[c, slot - 1])
+
+    def ow_relays(pairs):
+        for half, b in pairs:
+            gather_relay(ow_half, half, b, S_OG, og_r, oc_r)
 
     all_text = n_seq * text
     with jax.named_scope("attend"):
@@ -385,10 +398,31 @@
                 ).astype(BF16)
             for way in (1, -1):
                 reach(way, c, 1)
-
-    def ow_relays(pairs):
-        for half, b in pairs:
-            gather_relay(ow_half, half, b, S_OG, og_r, oc_r)
+            if c == OW_FIRST:
+                ow_relays(first)
+
+    cols = owg.shape[3]
+    part_width = mod_out.shape[1]
+    last = z + 1 - (2 * z) // n_head
+
+    def projection(at, j, slot):
+        return jnp.dot(
+            attg[slot, at], owg[j, lax.rem(z + n_head - slot, n_head)], preferred_element_type=F32
+        )
+
+    def accumulate(c):
+        at = cuts[c]
+        with jax.named_scope(f"accumulate{c}"):
+            for j in range(ratio):
+                here = slice(j * cols, (j + 1) * cols)
+                if vpart is None:
+                    base = vid[at, pl.ds(pl.multiple_of(z * part_width + j * cols, LANES), cols)]
+                else:
+                    base = vpart[at, here]
+                projected = projection(at, j, 0)
+                for i in range(1, n_head - 1):
+                    projected = projected + projection(at, j, lax.rem(last - 1 + i, n_head - 1) + 1)
+                acc[at, here] = base.astype(F32) + projected
 
     for d in range(1, n_head - 1):
         for c in range(chunks):
@@ -396,12 +430,21 @@
                 for way in (1, -1):
                     take(way, c, d)
                     reach(way, c, d + 1)
-            if d == 1 and c == 0:
-                with jax.named_scope("ow1"):
-                    ow_relays(first)
-            if d == 1 and c == chunks - 1:
+            if d == 1 and c == 1:
                 with jax.named_scope("ow2"):
                     ow_relays(second)
+            if d == n_head - 2 and c == 0:
+                with jax.named_scope("ow3"):
+                    for k in far:
+                        for half in range(2):
+                            gather_relay(ow_half, half, k, S_OG, og_r, oc_r)
+            if d == n_head - 2 and c == 1:
+                with jax.named_scope("ow4"):
+                    for k in [0] + masks:
+                        arrived(ow_slot(flip(s, k + 1)), oc_r.at[k // 2])
+            if d == n_head - 2 and c >= 1:
+                accumulate(c - 1)
+    accumulate(chunks - 1)
     with jax.named_scope("left1"):
         few = pl.ds(0, n_chip - 1)
         left(ctxg.at[few, ctx_rows(0)], send_sem.at[S_CTX])
@@ -416,16 +459,6 @@
         left(vall.at[pl.ds(0, n_seq - 1)], send_sem.at[S_V])
         left(kall.at[pl.ds(0, n_seq - 1)], send_sem.at[S_K])
         left(owg.at[:, pl.ds(0, n_head - 1), ow_piece(0), :], send_sem.at[S_OZ])
-    with jax.named_scope("ow3"):
-        for k in far:
-            for half in range(2):
-                gather_relay(ow_half, half, k, S_OG, og_r, oc_r)
-        for k in [0] + masks:
-            arrived(ow_slot(flip(s, k + 1)), oc_r.at[k // 2])
-
-    cols = owg.shape[3]
-    part_width = mod_out.shape[1]
-
     def modulate(c):
         at = cuts[c]
         step = at.stop - at.start
@@ -453,17 +486,7 @@
             row_sq = jnp.zeros((step, 1), F32)
             for j in range(ratio):
                 here = slice(j * cols, (j + 1) * cols)
-                projected = jnp.dot(attg[0, at], owg[j, z], preferred_element_type=F32)
-                for k in range(1, n_head):
-                    projected = projected + jnp.dot(
-                        attg[k, at], owg[j, lax.rem(z + n_head - k, n_head)],
-                        preferred_element_type=F32,
-                    )
-                if vpart is None:
-                    base = vid[at, pl.ds(pl.multiple_of(z * part_width + j * cols, LANES), cols)]
-                else:
-                    base = vpart[at, here]
-                rounded = (base.astype(F32) + projected).astype(BF16)
+                rounded = (acc[at, here] + projection(at, j, last)).astype(BF16)
                 resid_out[at, here] = rounded
                 wide = rounded.astype(F32)
                 row_sum = row_sum + jnp.sum(wide, axis=1, keepdims=True)
@@ -487,12 +510,17 @@
 
 
 def put_out(resid, mod, resid_hbm, mod_hbm, sems):
-    first = pltpu.make_async_copy(resid, resid_hbm, sems.at[0])
-    second = pltpu.make_async_copy(mod, mod_hbm, sems.at[1])
-    first.start()
-    second.start()
-    first.wait()
-    second.wait()
+    pieces = sems.shape[1]
+    rows = resid.shape[0] // pieces
+    copies = [
+        pltpu.make_async_copy(src.at[at], dst.at[at], sems.at[i, p])
+        for p, at in enumerate(pl.ds(p * rows, rows) for p in range(pieces))
+        for i, (src, dst) in enumerate(((resid, resid_hbm), (mod, mod_hbm)))
+    ]
+    for copy in copies:
+        copy.start()
+    for copy in copies:
+        copy.wait()
 
 
 def on_device(
@@ -519,7 +547,7 @@
     ratio = n_seq // n_head
     n_chip = n_seq // 2
     quarter = tok // 4
-    sizes = [quarter] * 3 + [quarter // 2] * 2
+    sizes = [quarter // 2] + [quarter] * 3 + [quarter // 2]
     cuts = [slice(sum(sizes[:c]), sum(sizes[: c + 1])) for c in range(len(sizes))]
     chunks = len(cuts)
     piece = out_weight.shape[0] // n_seq
@@ -540,9 +568,7 @@
     results = pl.pallas_call(
         functools.partial(body, n_seq, n_head, cuts, sliced),
         out_shape=[pltpu.VMEM((tok, part_width), BF16)] * 2,
-        in_specs=[pl.BlockSpec(memory_space=pltpu.SMEM)] * 2
-        + [hbm] * 11
-        + [vmem] * len(extra),
+        in_specs=[hbm] * 13 + [vmem] * len(extra),
         out_specs=[vmem] * 2,
         scratch_shapes=[
             pltpu.VMEM((tok, width), BF16),
@@ -563,14 +589,17 @@
             pltpu.VMEM((tok, att), F32),
             pltpu.VMEM((n_head, 1, tok), F32),
             pltpu.VMEM((n_head, 1, -(-text // LANES) * LANES), F32),
-            pltpu.VMEM((chunks, n_head, 2, LANES), F32),
+            pltpu.VMEM((chunks, n_head, 2, -(-max(sizes) // LANES) * LANES), F32),
             pltpu.VMEM((2, 8, part_width), F32),
             pltpu.VMEM(time_weight.shape, BF16),
             pltpu.VMEM((1, att), F32),
             pltpu.VMEM((1, att), F32),
             pltpu.VMEM((1, half), F32),
             pltpu.VMEM(modulation.shape, F32),
-            dma((12,)),
+            pltpu.VMEM((tok, part_width), F32),
+            pltpu.SMEM((1,), jnp.int32),
+            pltpu.SMEM((1,), jnp.int32),
+            dma((14,)),
             dma((14,)),
             dma((2, n_head - 1)),
             *[dma((n_chip,))] * 2,
@@ -603,7 +632,7 @@
         out_shape=[jax.ShapeDtypeStruct((tok, part_width), BF16)] * 2,
         in_specs=[vmem] * 2,
         out_specs=[hbm] * 2,
-        scratch_shapes=[dma((2,))],
+        scratch_shapes=[dma((2, 4))],
         compiler_params=pltpu.CompilerParams(vmem_limit_bytes=4 * 1024 * 1024),
     )(*results)
 

time: 64.8 us -> 64 us (0.988)
  Pallas kernels: 62.7 us -> 61.8 us
    pallas_call x1, Pallas kernels: 61.2 us -> 60.3 us  [on_device(): pl.pallas_call(functools.partial(body, n_seq, n_head, cuts, sliced), out_...]
where the time goes in v3:
time: 64 us; the launch traced here: 63.8 us
  Pallas kernels  61.8 us (97%)
  between operations  1.93 us (3%)
    pallas_call x1, Pallas kernels, on_device(): pl.pallas_call(functools.partial(body, n_seq, n_head, cuts, sliced), out_...  60.3 us
    pallas_call x1, Pallas kernels, on_device(): pl.pallas_call(put_out, out_shape=[jax.ShapeDtypeStruct((tok, part_width)...  1.55 us

profile of v3, /device:TPU:0, one launch (start us, length us, event | category | flops | bytes accessed | tf_op | source)
XLA Modules:
  0.0 63.8 jit_solution(5052663089101681127)
XLA Ops:
  1.9 60.3 %shard_map.140 = (bf16[512,1280]{1,0:T(8,128)(2,1)S(1)}, bf16[512,1280]{1,0:T(8,128)(2,1)S(1)}) custom-call(s32[1]{0:T(128)S(6)} %copy.15.refs_0_, s32[1]{0:T(128)S(6)} %copy.16.refs_1_, bf16[512,5120]{1,0:T(8,128)(2,1)} %refs_2_.1, bf16[64,5120]{1,0:T(8,128)(2,1)} %refs_3_.1, bf16[640,256]{1,0:T(8,128)(2,1)} %refs_4_.1, bf16[640,256]{1,0:T(8,128)(2,1)} %refs_5_.1, ...), custom_call_target="tpu_custom_call" | custom-call | tf_op jit(solution)/shard_map/pallas_call | solution.py:568
  62.2 1.5 %shard_map.141 = (bf16[512,1280]{1,0:T(8,128)(2,1)}, bf16[512,1280]{1,0:T(8,128)(2,1)}) custom-call(bf16[512,1280]{1,0:T(8,128)(2,1)S(1)} %get-tuple-element.4.resid, bf16[512,1280]{1,0:T(8,128)(2,1)S(1)} %get-tuple-element.5.mod), custom_call_target="tpu_custom_call" | custom-call | tf_op jit(solution)/shard_map/pallas_call | solution.py:630

commit v4 on v3

--- a/solution.py
+++ b/solution.py
@@ -12,7 +12,7 @@
 FREQ = 256
 LANES = 128
 VMEM_MOST = 67_000_000
-NORM_FIRST = 9
+NORM_AT = (5, 8)
 OW_FIRST = 3
 F32 = jnp.float32
 BF16 = jnp.bfloat16
@@ -174,7 +174,7 @@
 
     mine = z % 2
     own_ctx.wait()
-    for k in far + chip_bits:
+    for k in masks:
         push(
             ctxv.at[ctx_rows(mine), ctx_cols(flip(chip, k // 2))], ctxg.at[k // 2, ctx_rows(mine)],
             S_CTX, ctx_r.at[k // 2], to_seq(k),
@@ -206,13 +206,19 @@
                 spread_ = jnp.mean(centred * centred, axis=-1, keepdims=True)
                 normed[at, :] = (centred * (1.0 / jnp.sqrt(spread_ + 1e-06))).astype(BF16)
 
-    norm(0, strips * NORM_FIRST // 16)
-    with jax.named_scope("ctx_share"):
-        for k in far + chip_bits:
-            here = ctxg.at[k // 2, ctx_rows(mine)]
-            arrived(here, ctx_r.at[k // 2])
-            push(here, here, S_CTZ, ctz_r.at[k // 2], to_head(1))
-    norm(strips * NORM_FIRST // 16, strips)
+    def share(ks):
+        with jax.named_scope("share%d" % len(ks)):
+            for k in ks:
+                here = ctxg.at[k // 2, ctx_rows(mine)]
+                arrived(here, ctx_r.at[k // 2])
+                push(here, here, S_CTZ, ctz_r.at[k // 2], to_head(1))
+
+    done = [strips * n // 16 for n in NORM_AT]
+    norm(0, done[0])
+    share(chip_bits)
+    norm(done[0], done[1])
+    share(far)
+    norm(done[1], strips)
 
     with jax.named_scope("kv"):
         arrived(kvw.at[1 - core], one_r.at[R_W])
@@ -223,24 +229,27 @@
         block = partial_kv(ctxv[:, ctx_cols(chip)])
         cks[0] = block[:, :att]
         ckr[0] = block[:, att:]
-        for k in far + chip_bits:
+        for k in masks:
             c = k // 2
             arrived(ctxg.at[c, ctx_rows(1 - mine)], ctz_r.at[c])
             block = partial_kv(ctxg[c])
             cks[c] = block[:, :att]
             cvs[c] = block[:, att:].astype(BF16)
             push(cks.at[c], ckr.at[c], S_CK, one_r.at[R_CK], to_seq(k))
-        for k in far + chip_bits:
-            c = k // 2
-            push(cvs.at[c], cvr.at[c], S_CV, one_r.at[R_CV], to_seq(k))
+
+    def shard_queries(p, rows):
+        lanes = pl.ds(pl.multiple_of(p * rows, rows), rows)
+        return jnp.dot(normed[:, lanes], qwg[lanes, :], preferred_element_type=F32)
 
     def chip_queries(p):
-        lanes = pl.ds(pl.multiple_of(p * pair, pair), pair)
-        return jnp.dot(normed[:, lanes], qwg[lanes, :], preferred_element_type=F32)
+        return shard_queries(p, pair)
 
     with jax.named_scope("relay1"):
         for half, b in first:
             gather_relay(half_rows, half, b, S_QW, qw_r, qc_r)
+        for k in masks:
+            c = k // 2
+            push(cvs.at[c], cvr.at[c], S_CV, one_r.at[R_CV], to_seq(k))
 
     def own_cols(zz):
         return pl.ds(zz * ratio, ratio)
@@ -265,7 +274,7 @@
         own_tw.wait()
         for copy in small:
             copy.wait()
-        angles = jnp.broadcast_to(when[0].astype(F32) * freqs[...], (16, freqs.shape[1]))
+        angles = jnp.broadcast_to(when[...].astype(F32) * freqs[...], (16, freqs.shape[1]))
         embedding = jnp.concatenate([jnp.cos(angles), jnp.sin(angles)], axis=1)
         act = (embedding / (1.0 + jnp.exp(-embedding))).astype(BF16)
         for i in range(2):
@@ -280,6 +289,26 @@
         ksq[0] = column_to_row(jnp.sum(key_rows * key_rows, axis=1, keepdims=True))
         for k in range(1, n_head):
             push(ksq.at[0], ksq.at[k], S_KSQ, one_r.at[R_KSQ], to_head(k))
+
+    with jax.named_scope("q_mid"):
+        for b in chip_bits:
+            arrived(shard_rows(flip(s, b + 1)), qc_r.at[b // 2])
+            queries[...] += chip_queries(flip(chip, b // 2))
+
+    with jax.named_scope("far_relay"):
+        for k in far:
+            for half in range(2):
+                gather_relay(half_rows, half, k, S_QW, qw_r, qc_r)
+
+    with jax.named_scope("k_norm"):
+        arrived(ksq.at[pl.ds(1, n_head - 1)], one_r.at[R_KSQ])
+        k_mean = row_to_column(jnp.sum(ksq[...], axis=0), text) / (att * n_head)
+        kall[s] = (cks[0] / jnp.sqrt(k_mean + 1e-06) * kg[...]).astype(BF16)
+        for k in masks:
+            push(kall.at[s], kall.at[s], S_K, one_r.at[R_K], to_seq(k))
+        push(kall.at[s], kall.at[s], S_K, one_r.at[R_KC], to_seq(1))
+
+    with jax.named_scope("v_sum"):
         arrived(cvr.at[pl.ds(1, n_chip - 1)], one_r.at[R_CV])
         value_rows = ckr[0]
         for c in range(1, n_chip):
@@ -289,19 +318,6 @@
             push(vall.at[s], vall.at[s], S_V, one_r.at[R_V], to_seq(k))
         push(vall.at[s], vall.at[s], S_V, one_r.at[R_VC], to_seq(1))
 
-    with jax.named_scope("q_mid"):
-        for b in chip_bits:
-            arrived(shard_rows(flip(s, b + 1)), qc_r.at[b // 2])
-            queries[...] += chip_queries(flip(chip, b // 2))
-
-    with jax.named_scope("k_norm"):
-        arrived(ksq.at[pl.ds(1, n_head - 1)], one_r.at[R_KSQ])
-        k_mean = row_to_column(jnp.sum(ksq[...], axis=0), text) / (att * n_head)
-        kall[s] = (cks[0] / jnp.sqrt(k_mean + 1e-06) * kg[...]).astype(BF16)
-        for k in masks:
-            push(kall.at[s], kall.at[s], S_K, one_r.at[R_K], to_seq(k))
-        push(kall.at[s], kall.at[s], S_K, one_r.at[R_KC], to_seq(1))
-
     def ow_half(half, p):
         if ratio == 1:
             rows = piece // 2
@@ -312,38 +328,40 @@
     def ow_slot(p):
         return owg.at[:, :, ow_piece(p), :]
 
+    with jax.named_scope("q_far"):
+        for k in far:
+            if depth % LANES == 0:
+                queries[...] += shard_queries(flip(s, k), depth)
+            arrived(shard_rows(flip(s, k + 1)), qc_r.at[k // 2])
+            if depth % LANES == 0:
+                queries[...] += shard_queries(flip(s, k + 1), depth)
+            else:
+                queries[...] += chip_queries(flip(chip, k // 2))
+        q = queries[...]
+        qsq[0] = column_to_row(jnp.sum(q * q, axis=1, keepdims=True))
+        for k in range(1, n_head):
+            push(qsq.at[0], qsq.at[k], S_QSQ, one_r.at[R_QSQ], to_head(k))
+
+    with jax.named_scope("kv_in"):
+        for ref, group, chips in ((kall, S_K, R_K), (vall, S_V, R_V)):
+            arrived(ref.at[pl.ds(0, n_chip - 1)], one_r.at[chips])
+            for k in masks:
+                here = ref.at[flip(s, k)]
+                push(here, here, group, one_r.at[chips + 1], to_seq(1))
     with jax.named_scope("ow_start"):
         own_ow.wait()
         arrived(owg.at[:, pl.ds(0, n_head - 1), ow_piece(s), :], one_r.at[R_OZ])
         for half, b in first + second:
             gather_own(ow_half, half, [b], S_OG, og_r)
         gather_core(ow_half, S_OG, oc_r)
-
-    with jax.named_scope("q_far"):
-        for k in far:
-            for half in range(2):
-                gather_relay(half_rows, half, k, S_QW, qw_r, qc_r)
-        for k in far:
-            arrived(shard_rows(flip(s, k + 1)), qc_r.at[k // 2])
-            queries[...] += chip_queries(flip(chip, k // 2))
-        q = queries[...]
-        qsq[0] = column_to_row(jnp.sum(q * q, axis=1, keepdims=True))
-        for k in range(1, n_head):
-            push(qsq.at[0], qsq.at[k], S_QSQ, one_r.at[R_QSQ], to_head(k))
-
-    with jax.named_scope("kv_in"):
-        for ref, group, chips in ((vall, S_V, R_V), (kall, S_K, R_K)):
-            arrived(ref.at[pl.ds(0, n_chip - 1)], one_r.at[chips])
-            for k in masks:
-                here = ref.at[flip(s, k)]
-                push(here, here, group, one_r.at[chips + 1], to_seq(1))
+    with jax.named_scope("kv_end"):
         for ref, chips in ((vall, R_V), (kall, R_K)):
             arrived(ref.at[pl.ds(0, n_chip)], one_r.at[chips + 1])
 
     with jax.named_scope("q_norm"):
         arrived(qsq.at[pl.ds(1, n_head - 1)], one_r.at[R_QSQ])
         q_mean = row_to_column(jnp.sum(qsq[...], axis=0), tok) / (att * n_head)
-        q_normed = (queries[...] / jnp.sqrt(q_mean + 1e-06) * qg[...]).astype(BF16)
+        q_root = jnp.sqrt(q_mean + 1e-06)
 
     def held(way, d):
         return d % n_head if way > 0 else (n_head - d) % n_head
@@ -381,13 +399,14 @@
     with jax.named_scope("attend"):
         every_k = kall[...].reshape(all_text, att)
         every_v = vall[...].reshape(all_text, att)
-        seen = lax.broadcasted_iota(jnp.int32, (1, all_text), 1) < valid[0]
+        seen = lax.broadcasted_iota(jnp.int32, (1, all_text), 1) < valid[...]
         for c in range(chunks):
             at = cuts[c]
+            q_normed = (queries[at, :] / q_root[at] * qg[...]).astype(BF16)
             for h in range(att // HD):
                 lanes = slice(h * HD, (h + 1) * HD)
                 scores = lax.dot_general(
-                    q_normed[at, lanes], every_k[:, lanes], (((1,), (1,)), ((), ())),
+                    q_normed[:, lanes], every_k[:, lanes], (((1,), (1,)), ((), ())),
                     preferred_element_type=F32,
                 ) * HD ** (-0.5)
                 scores = jnp.where(seen, scores, F32(-1e30))
@@ -597,8 +616,8 @@
             pltpu.VMEM((1, half), F32),
             pltpu.VMEM(modulation.shape, F32),
             pltpu.VMEM((tok, part_width), F32),
-            pltpu.SMEM((1,), jnp.int32),
-            pltpu.SMEM((1,), jnp.int32),
+            pltpu.VMEM((1, 1), jnp.int32),
+            pltpu.VMEM((1, 1), jnp.int32),
             dma((14,)),
             dma((14,)),
             dma((2, n_head - 1)),
@@ -612,8 +631,8 @@
             collective_id=0, has_side_effects=True, vmem_limit_bytes=VMEM_MOST - 2 * out_bytes
         ),
     )(
-        valid_length,
-        timestep,
+        valid_length[None, :],
+        timestep[None, :],
         video_rows,
         context,
         query_weight,

time: 64 us -> 63.4 us (level)
  no operation moved by 1% of the time
where the time goes in v4:
time: 63.4 us; the launch traced here: 63.2 us
  Pallas kernels  61.3 us (97%)
  between operations  1.93 us (3%)
    pallas_call x1, Pallas kernels, on_device(): pl.pallas_call(functools.partial(body, n_seq, n_head, cuts, sliced), out_...  59.7 us
    pallas_call x1, Pallas kernels, on_device(): pl.pallas_call(put_out, out_shape=[jax.ShapeDtypeStruct((tok, part_width)...  1.55 us

profile of v4, /device:TPU:0, one launch (start us, length us, event | category | flops | bytes accessed | tf_op | source)
XLA Modules:
  0.0 63.2 jit_solution(10059497126848012483)
XLA Ops:
  1.9 59.7 %shard_map.140 = (bf16[512,1280]{1,0:T(8,128)(2,1)S(1)}, bf16[512,1280]{1,0:T(8,128)(2,1)S(1)}) custom-call(s32[1,1]{1,0:T(1,128)} %bitcast.4.refs_0_, s32[1,1]{1,0:T(1,128)} %bitcast.5.refs_1_, bf16[512,5120]{1,0:T(8,128)(2,1)} %refs_2_.1, bf16[64,5120]{1,0:T(8,128)(2,1)} %refs_3_.1, bf16[640,256]{1,0:T(8,128)(2,1)} %refs_4_.1, bf16[640,256]{1,0:T(8,128)(2,1)} %refs_5_.1, ...), custom_call_target="tpu_custom_call" | custom-call | tf_op jit(solution)/shard_map/pallas_call | solution.py:587
  61.6 1.5 %shard_map.141 = (bf16[512,1280]{1,0:T(8,128)(2,1)}, bf16[512,1280]{1,0:T(8,128)(2,1)}) custom-call(bf16[512,1280]{1,0:T(8,128)(2,1)S(1)} %get-tuple-element.4.resid, bf16[512,1280]{1,0:T(8,128)(2,1)S(1)} %get-tuple-element.5.mod), custom_call_target="tpu_custom_call" | custom-call | tf_op jit(solution)/shard_map/pallas_call | solution.py:649

commit v5 on v4

--- a/solution.py
+++ b/solution.py
@@ -13,7 +13,6 @@
 LANES = 128
 VMEM_MOST = 67_000_000
 NORM_AT = (5, 8)
-OW_FIRST = 3
 F32 = jnp.float32
 BF16 = jnp.bfloat16
 MESH_ID = pl.DeviceIdType.MESH
@@ -63,7 +62,7 @@
     n_seq, n_head, cuts,
     valid_hbm, when_hbm, video, ctx, qw, kw, vw, ow, qg_hbm, kg_hbm, freqs_hbm, tw_hbm, mod_hbm, vpart,
     resid_out, mod_out,
-    vid, normed, ctxv, ctxg, qwg, kvw, cks, ckr, cvs, cvr, kall, vall, spread, owg, attg,
+    vid, normed, ctxv, ctxg, qwg, kvw, cks, ckr, cvs, cvr, own_v, key_sum, kall, vall, spread, owg, attg,
     queries, qsq, ksq, stat, shsc, tw, qg, kg, freqs, mod, acc, valid, when,
     loc_sem, send_sem, pass_s, ctx_r, ctz_r, qw_r, qc_r, og_r, oc_r, at_r, st_r, one_r,
 ):
@@ -220,6 +219,18 @@
     share(far)
     norm(done[1], strips)
 
+    def keeper(k):
+        return (flip(s, k) // 2 * 2 + 1, z)
+
+    def chip_slot(ref, p):
+        return ref.at[pl.ds(2 * p, 2)]
+
+    def spread_text(ref, group, chips):
+        here = chip_slot(ref, chip)
+        for k in masks:
+            push(here, here, group, one_r.at[chips], to_seq(k))
+        push(here, here, group, one_r.at[chips + 1], to_seq(1))
+
     with jax.named_scope("kv"):
         arrived(kvw.at[1 - core], one_r.at[R_W])
 
@@ -228,14 +239,19 @@
 
         block = partial_kv(ctxv[:, ctx_cols(chip)])
         cks[0] = block[:, :att]
-        ckr[0] = block[:, att:]
+        own_v[...] = block[:, att:]
+        cvs[0] = block[:, att:].astype(BF16)
         for k in masks:
             c = k // 2
             arrived(ctxg.at[c, ctx_rows(1 - mine)], ctz_r.at[c])
             block = partial_kv(ctxg[c])
             cks[c] = block[:, :att]
             cvs[c] = block[:, att:].astype(BF16)
-            push(cks.at[c], ckr.at[c], S_CK, one_r.at[R_CK], to_seq(k))
+            push(cks.at[c], ckr.at[core * n_chip + c], S_CK, one_r.at[R_CK], keeper(k))
+
+        @pl.when(core == 0)
+        def _():
+            push(cks.at[0], ckr.at[0], S_CK, one_r.at[R_CK], to_seq(1))
 
     def shard_queries(p, rows):
         lanes = pl.ds(pl.multiple_of(p * rows, rows), rows)
@@ -249,7 +265,11 @@
             gather_relay(half_rows, half, b, S_QW, qw_r, qc_r)
         for k in masks:
             c = k // 2
-            push(cvs.at[c], cvr.at[c], S_CV, one_r.at[R_CV], to_seq(k))
+            push(cvs.at[c], cvr.at[core * n_chip + c], S_CV, one_r.at[R_CV], keeper(k))
+
+        @pl.when(core == 0)
+        def _():
+            push(cvs.at[0], cvr.at[0], S_CV, one_r.at[R_CV], to_seq(1))
 
     def own_cols(zz):
         return pl.ds(zz * ratio, ratio)
@@ -280,15 +300,19 @@
         for i in range(2):
             shsc[i] = mod[i : i + 1, :] + jnp.dot(act, tw[i], preferred_element_type=F32)[:8]
 
-    with jax.named_scope("kv_sum"):
-        arrived(ckr.at[pl.ds(1, n_chip - 1)], one_r.at[R_CK])
-        key_rows = cks[0]
-        for c in range(1, n_chip):
-            key_rows = key_rows + ckr[c]
-        cks[0] = key_rows
-        ksq[0] = column_to_row(jnp.sum(key_rows * key_rows, axis=1, keepdims=True))
-        for k in range(1, n_head):
-            push(ksq.at[0], ksq.at[k], S_KSQ, one_r.at[R_KSQ], to_head(k))
+    @pl.when(core == 1)
+    def _():
+        with jax.named_scope("kv_sum"):
+            arrived(ckr.at[pl.ds(0, n_seq - 1)], one_r.at[R_CK])
+            both = [ckr[0], cks[0]]
+            for q in range(2):
+                for c in range(1, n_chip):
+                    both[q] = both[q] + ckr[q * n_chip + c]
+            key_rows = jnp.concatenate(both, axis=0)
+            key_sum[...] = key_rows
+            ksq[0] = column_to_row(jnp.sum(key_rows * key_rows, axis=1, keepdims=True))
+            for k in range(1, n_head):
+                push(ksq.at[0], ksq.at[k], S_KSQ, one_r.at[R_KSQ], to_head(k))
 
     with jax.named_scope("q_mid"):
         for b in chip_bits:
@@ -300,23 +324,23 @@
             for half in range(2):
                 gather_relay(half_rows, half, k, S_QW, qw_r, qc_r)
 
-    with jax.named_scope("k_norm"):
-        arrived(ksq.at[pl.ds(1, n_head - 1)], one_r.at[R_KSQ])
-        k_mean = row_to_column(jnp.sum(ksq[...], axis=0), text) / (att * n_head)
-        kall[s] = (cks[0] / jnp.sqrt(k_mean + 1e-06) * kg[...]).astype(BF16)
-        for k in masks:
-            push(kall.at[s], kall.at[s], S_K, one_r.at[R_K], to_seq(k))
-        push(kall.at[s], kall.at[s], S_K, one_r.at[R_KC], to_seq(1))
-
-    with jax.named_scope("v_sum"):
-        arrived(cvr.at[pl.ds(1, n_chip - 1)], one_r.at[R_CV])
-        value_rows = ckr[0]
-        for c in range(1, n_chip):
-            value_rows = value_rows + cvr[c].astype(F32)
-        vall[s] = value_rows.astype(BF16)
-        for k in masks:
-            push(vall.at[s], vall.at[s], S_V, one_r.at[R_V], to_seq(k))
-        push(vall.at[s], vall.at[s], S_V, one_r.at[R_VC], to_seq(1))
+    @pl.when(core == 1)
+    def _():
+        with jax.named_scope("k_norm"):
+            arrived(ksq.at[pl.ds(1, n_head - 1)], one_r.at[R_KSQ])
+            k_mean = row_to_column(jnp.sum(ksq[...], axis=0), 2 * text) / (att * n_head)
+            key_normed = (key_sum[...] / jnp.sqrt(k_mean + 1e-06) * kg[...]).astype(BF16)
+            for q in range(2):
+                kall[2 * chip + q] = key_normed[q * text : (q + 1) * text]
+            spread_text(kall, S_K, R_K)
+        with jax.named_scope("v_sum"):
+            arrived(cvr.at[pl.ds(0, n_seq - 1)], one_r.at[R_CV])
+            both = [cvr[0].astype(F32), own_v[...]]
+            for q in range(2):
+                for c in range(1, n_chip):
+                    both[q] = both[q] + cvr[q * n_chip + c].astype(F32)
+                vall[2 * chip + q] = both[q].astype(BF16)
+            spread_text(vall, S_V, R_V)
 
     def ow_half(half, p):
         if ratio == 1:
@@ -342,21 +366,27 @@
         for k in range(1, n_head):
             push(qsq.at[0], qsq.at[k], S_QSQ, one_r.at[R_QSQ], to_head(k))
 
-    with jax.named_scope("kv_in"):
-        for ref, group, chips in ((kall, S_K, R_K), (vall, S_V, R_V)):
-            arrived(ref.at[pl.ds(0, n_chip - 1)], one_r.at[chips])
-            for k in masks:
-                here = ref.at[flip(s, k)]
-                push(here, here, group, one_r.at[chips + 1], to_seq(1))
+    @pl.when(core == 1)
+    def _():
+        with jax.named_scope("kv_in"):
+            for ref, group, chips in ((kall, S_K, R_K), (vall, S_V, R_V)):
+                arrived(ref.at[pl.ds(0, n_seq - 2)], one_r.at[chips])
+                for k in masks:
+                    here = chip_slot(ref, flip(chip, k // 2))
+                    push(here, here, group, one_r.at[chips + 1], to_seq(1))
+
+    @pl.when(core == 0)
+    def _():
+        with jax.named_scope("kv_end"):
+            for ref, chips in ((kall, R_K), (vall, R_V)):
+                arrived(ref, one_r.at[chips + 1])
+
     with jax.named_scope("ow_start"):
         own_ow.wait()
         arrived(owg.at[:, pl.ds(0, n_head - 1), ow_piece(s), :], one_r.at[R_OZ])
         for half, b in first + second:
             gather_own(ow_half, half, [b], S_OG, og_r)
         gather_core(ow_half, S_OG, oc_r)
-    with jax.named_scope("kv_end"):
-        for ref, chips in ((vall, R_V), (kall, R_K)):
-            arrived(ref.at[pl.ds(0, n_chip)], one_r.at[chips + 1])
 
     with jax.named_scope("q_norm"):
         arrived(qsq.at[pl.ds(1, n_head - 1)], one_r.at[R_QSQ])
@@ -417,8 +447,6 @@
                 ).astype(BF16)
             for way in (1, -1):
                 reach(way, c, 1)
-            if c == OW_FIRST:
-                ow_relays(first)
 
     cols = owg.shape[3]
     part_width = mod_out.shape[1]
@@ -429,9 +457,9 @@
             attg[slot, at], owg[j, lax.rem(z + n_head - slot, n_head)], preferred_element_type=F32
         )
 
-    def accumulate(c):
-        at = cuts[c]
-        with jax.named_scope(f"accumulate{c}"):
+    def accumulate(begin, end):
+        at = slice(cuts[begin].start, cuts[end - 1].stop)
+        with jax.named_scope(f"accumulate{begin}"):
             for j in range(ratio):
                 here = slice(j * cols, (j + 1) * cols)
                 if vpart is None:
@@ -450,20 +478,22 @@
                     take(way, c, d)
                     reach(way, c, d + 1)
             if d == 1 and c == 1:
+                with jax.named_scope("ow1"):
+                    ow_relays(first)
+            if d == 1 and c == chunks - 1:
                 with jax.named_scope("ow2"):
                     ow_relays(second)
-            if d == n_head - 2 and c == 0:
+            if d == n_head - 2 and c == 1:
                 with jax.named_scope("ow3"):
                     for k in far:
                         for half in range(2):
                             gather_relay(ow_half, half, k, S_OG, og_r, oc_r)
-            if d == n_head - 2 and c == 1:
+            if d == n_head - 2 and c == 2:
                 with jax.named_scope("ow4"):
                     for k in [0] + masks:
                         arrived(ow_slot(flip(s, k + 1)), oc_r.at[k // 2])
-            if d == n_head - 2 and c >= 1:
-                accumulate(c - 1)
-    accumulate(chunks - 1)
+                accumulate(0, 3)
+    accumulate(3, chunks)
     with jax.named_scope("left1"):
         few = pl.ds(0, n_chip - 1)
         left(ctxg.at[few, ctx_rows(0)], send_sem.at[S_CTX])
@@ -471,13 +501,22 @@
         left(kvw.at[0], send_sem.at[S_W])
         left(spread.at[pl.ds(0, n_seq - 1)], send_sem.at[S_SP])
         left(shard_rows(0, n_seq - 1), send_sem.at[S_QW])
-        left(ckr.at[few], send_sem.at[S_CK])
-        left(cvr.at[few], send_sem.at[S_CV])
-        left(ksq.at[pl.ds(0, n_head - 1)], send_sem.at[S_KSQ])
         left(qsq.at[pl.ds(0, n_head - 1)], send_sem.at[S_QSQ])
-        left(vall.at[pl.ds(0, n_seq - 1)], send_sem.at[S_V])
-        left(kall.at[pl.ds(0, n_seq - 1)], send_sem.at[S_K])
         left(owg.at[:, pl.ds(0, n_head - 1), ow_piece(0), :], send_sem.at[S_OZ])
+
+        @pl.when(core == 0)
+        def _():
+            left(ckr.at[pl.ds(0, n_chip)], send_sem.at[S_CK])
+            left(cvr.at[pl.ds(0, n_chip)], send_sem.at[S_CV])
+
+        @pl.when(core == 1)
+        def _():
+            left(ckr.at[few], send_sem.at[S_CK])
+            left(cvr.at[few], send_sem.at[S_CV])
+            left(ksq.at[pl.ds(0, n_head - 1)], send_sem.at[S_KSQ])
+            for group in (S_V, S_K):
+                left(qwg.at[pl.ds(0, 2 * (n_seq - 1) * text)], send_sem.at[group])
+
     def modulate(c):
         at = cuts[c]
         step = at.stop - at.start
@@ -514,8 +553,6 @@
             stat[c, 0, 1:] = column_to_row(row_sq)
             for k in range(1, n_head):
                 push(stat.at[c, 0], stat.at[c, k], S_ST, st_r.at[c], to_head(k))
-        if c >= 3:
-            modulate(c - 3)
     with jax.named_scope("left2"):
         left(owg.at[:, :, pl.ds(0, piece * (n_seq - 1)), :], send_sem.at[S_OG])
         for way in (1, -1):
@@ -523,7 +560,7 @@
                 @pl.when(onward(way, d))
                 def _():
                     left(attg.at[0], passed(way, d))
-    for c in range(max(chunks - 3, 0), chunks):
+    for c in range(chunks):
         modulate(c)
     left(stat.at[:, pl.ds(0, n_head - 1)], send_sem.at[S_ST])
 
@@ -597,9 +634,11 @@
             pltpu.VMEM((n_seq * depth, att), BF16),
             pltpu.VMEM((2, depth, 2 * att), BF16),
             pltpu.VMEM((n_chip, text, att), F32),
-            pltpu.VMEM((n_chip, text, att), F32),
+            pltpu.VMEM((n_seq, text, att), F32),
             pltpu.VMEM((n_chip, text, att), BF16),
-            pltpu.VMEM((n_chip, text, att), BF16),
+            pltpu.VMEM((n_seq, text, att), BF16),
+            pltpu.VMEM((text, att), F32),
+            pltpu.VMEM((2 * text, att), F32),
             pltpu.VMEM((n_seq, text, att), BF16),
             pltpu.VMEM((n_seq, text, att), BF16),
             pltpu.VMEM((n_seq, piece, cols), BF16),
@@ -607,7 +646,7 @@
             pltpu.VMEM((n_head, tok, att), BF16),
             pltpu.VMEM((tok, att), F32),
             pltpu.VMEM((n_head, 1, tok), F32),
-            pltpu.VMEM((n_head, 1, -(-text // LANES) * LANES), F32),
+            pltpu.VMEM((n_head, 1, -(-2 * text // LANES) * LANES), F32),
             pltpu.VMEM((chunks, n_head, 2, -(-max(sizes) // LANES) * LANES), F32),
             pltpu.VMEM((2, 8, part_width), F32),
             pltpu.VMEM(time_weight.shape, BF16),

time: 63.4 us -> 62.3 us (0.983)
  Pallas kernels: 61.3 us -> 60.2 us
    pallas_call x1, Pallas kernels: 59.7 us -> 58.7 us  [on_device(): pl.pallas_call(functools.partial(body, n_seq, n_head, cuts, sliced), out_...]
where the time goes in v5:
time: 62.3 us; the launch traced here: 62.1 us
  Pallas kernels  60.2 us (97%)
  between operations  1.93 us (3%)
    pallas_call x1, Pallas kernels, on_device(): pl.pallas_call(functools.partial(body, n_seq, n_head, cuts, sliced), out_...  58.7 us
    pallas_call x1, Pallas kernels, on_device(): pl.pallas_call(put_out, out_shape=[jax.ShapeDtypeStruct((tok, part_width)...  1.55 us

profile of v5, /device:TPU:0, one launch (start us, length us, event | category | flops | bytes accessed | tf_op | source)
XLA Modules:
  0.0 62.1 jit_solution(11422797443539260115)
XLA Ops:
  1.9 58.7 %shard_map.140 = (bf16[512,1280]{1,0:T(8,128)(2,1)S(1)}, bf16[512,1280]{1,0:T(8,128)(2,1)S(1)}) custom-call(s32[1,1]{1,0:T(1,128)} %bitcast.4.refs_0_, s32[1,1]{1,0:T(1,128)} %bitcast.5.refs_1_, bf16[512,5120]{1,0:T(8,128)(2,1)} %refs_2_.1, bf16[64,5120]{1,0:T(8,128)(2,1)} %refs_3_.1, bf16[640,256]{1,0:T(8,128)(2,1)} %refs_4_.1, bf16[640,256]{1,0:T(8,128)(2,1)} %refs_5_.1, ...), custom_call_target="tpu_custom_call" | custom-call | tf_op jit(solution)/shard_map/pallas_call | solution.py:624
  60.6 1.5 %shard_map.141 = (bf16[512,1280]{1,0:T(8,128)(2,1)}, bf16[512,1280]{1,0:T(8,128)(2,1)}) custom-call(bf16[512,1280]{1,0:T(8,128)(2,1)S(1)} %get-tuple-element.4.resid, bf16[512,1280]{1,0:T(8,128)(2,1)S(1)} %get-tuple-element.5.mod), custom_call_target="tpu_custom_call" | custom-call | tf_op jit(solution)/shard_map/pallas_call | solution.py:688

commit v6 on v5

--- a/solution.py
+++ b/solution.py
@@ -12,7 +12,7 @@
 FREQ = 256
 LANES = 128
 VMEM_MOST = 67_000_000
-NORM_AT = (5, 8)
+NORM_AT = (6, 8, 9)
 F32 = jnp.float32
 BF16 = jnp.bfloat16
 MESH_ID = pl.DeviceIdType.MESH
@@ -81,8 +81,8 @@
     masks = by_hops(n_seq)
     chip_bits = [k for k in masks if len(bits_of(k)) == 1]
     far = [k for k in masks if k not in chip_bits]
-    (S_CTX, S_CTZ, S_W, S_SP, S_QW, S_CK, S_CV, S_KSQ, S_QSQ, S_V, S_K, S_OZ, S_OG, S_ST) = range(14)
-    (R_W, R_SP, R_CK, R_CV, R_KSQ, R_QSQ, R_V, R_VC, R_K, R_KC, R_OZ) = range(11)
+    (S_CTX, S_W, S_SP, S_QW, S_CK, S_CV, S_KSQ, S_QSQ, S_KV, S_OZ, S_OG, S_ST) = range(12)
+    (R_W, R_SP, R_CK, R_CV, R_KSQ, R_QSQ, R_V, R_VC, R_K, R_KC, R_OZ, R_SPL) = range(12)
 
     def to_seq(k):
         return (flip(s, k), z)
@@ -107,7 +107,7 @@
 
     def gather_own(slot, half, bits, group, rsem):
         for b in bits:
-            push(slot(half, s), slot(half, s), group, rsem.at[half, b // 2], to_seq(b))
+            push(slot(half, s), slot(half, s), group, rsem.at[half, b // 2 - 1], to_seq(b))
 
     def gather_core(slot, group, csem):
         for half in range(2):
@@ -115,10 +115,10 @@
 
     def gather_relay(slot, half, k, group, rsem, csem):
         here = slot(half, flip(s, k))
-        arrived(here, rsem.at[half, k // 2])
+        arrived(here, rsem.at[half, k // 2 - 1])
         for b in chip_bits:
             if not k & b and last_bit(half, k | b) == b:
-                push(here, here, group, rsem.at[half, (k | b) // 2], to_seq(b))
+                push(here, here, group, rsem.at[half, (k | b) // 2 - 1], to_seq(b))
         push(here, here, group, csem.at[k // 2], to_seq(1))
 
     barrier = pltpu.get_barrier_semaphore()
@@ -146,13 +146,13 @@
 
     own_ctx = load(ctx, ctxv, 0)
     own_qw = load(qw, shard_rows(s), 1)
-    own_kw = load(kw, kvw.at[core, :, :att], 2)
-    own_vw = load(vw, kvw.at[core, :, att:], 3)
+    load(kw, kvw.at[core, :, :att], 2)
+    load(vw, kvw.at[core, :, att:], 2)
     own_vid = load(video, vid, 4)
     own_spread = load(ow.at[ow_piece(s), :], spread.at[s], 5)
     own_tw = load(tw_hbm, tw, 6)
     small = [
-        load(a, b, 8 + i)
+        load(a, b, 7 + i)
         for i, (a, b) in enumerate(
             (
                 (qg_hbm, qg), (kg_hbm, kg), (freqs_hbm, freqs), (mod_hbm, mod),
@@ -176,13 +176,16 @@
     for k in masks:
         push(
             ctxv.at[ctx_rows(mine), ctx_cols(flip(chip, k // 2))], ctxg.at[k // 2, ctx_rows(mine)],
-            S_CTX, ctx_r.at[k // 2], to_seq(k),
+            S_CTX, ctx_r.at[k // 2 - 1], to_seq(k),
         )
-    own_kw.wait()
-    own_vw.wait()
+    pltpu.make_async_copy(kvw.at[core], kvw.at[core], loc_sem.at[2]).wait()
     push(kvw.at[core], kvw.at[core], S_W, one_r.at[R_W], to_seq(1))
-    for k in masks + [k + 1 for k in masks] + [1]:
-        push(ow.at[ow_piece(flip(s, k)), :], spread.at[s], S_SP, one_r.at[R_SP], to_seq(k))
+
+    def spread_rows(ks, rsem):
+        for k in ks:
+            push(ow.at[ow_piece(flip(s, k)), :], spread.at[s], S_SP, one_r.at[rsem], to_seq(k))
+
+    spread_rows(masks, R_SP)
     own_qw.wait()
     first = [(0, b) for b in chip_bits[:1]] + [(1, b) for b in chip_bits[1:]]
     second = [(0, b) for b in chip_bits[1:]] + [(1, b) for b in chip_bits[:1]]
@@ -209,15 +212,15 @@
         with jax.named_scope("share%d" % len(ks)):
             for k in ks:
                 here = ctxg.at[k // 2, ctx_rows(mine)]
-                arrived(here, ctx_r.at[k // 2])
-                push(here, here, S_CTZ, ctz_r.at[k // 2], to_head(1))
+                arrived(here, ctx_r.at[k // 2 - 1])
+                push(here, here, S_CTX, ctz_r.at[k // 2 - 1], to_head(1))
 
     done = [strips * n // 16 for n in NORM_AT]
     norm(0, done[0])
     share(chip_bits)
     norm(done[0], done[1])
     share(far)
-    norm(done[1], strips)
+    norm(done[1], done[2])
 
     def keeper(k):
         return (flip(s, k) // 2 * 2 + 1, z)
@@ -225,11 +228,11 @@
     def chip_slot(ref, p):
         return ref.at[pl.ds(2 * p, 2)]
 
-    def spread_text(ref, group, chips):
+    def spread_text(ref, chips):
         here = chip_slot(ref, chip)
         for k in masks:
-            push(here, here, group, one_r.at[chips], to_seq(k))
-        push(here, here, group, one_r.at[chips + 1], to_seq(1))
+            push(here, here, S_KV, one_r.at[chips], to_seq(k))
+        push(here, here, S_KV, one_r.at[chips + 1], to_seq(1))
 
     with jax.named_scope("kv"):
         arrived(kvw.at[1 - core], one_r.at[R_W])
@@ -243,7 +246,7 @@
         cvs[0] = block[:, att:].astype(BF16)
         for k in masks:
             c = k // 2
-            arrived(ctxg.at[c, ctx_rows(1 - mine)], ctz_r.at[c])
+            arrived(ctxg.at[c, ctx_rows(1 - mine)], ctz_r.at[c - 1])
             block = partial_kv(ctxg[c])
             cks[c] = block[:, :att]
             cvs[c] = block[:, att:].astype(BF16)
@@ -271,18 +274,28 @@
         def _():
             push(cvs.at[0], cvr.at[0], S_CV, one_r.at[R_CV], to_seq(1))
 
+    spread_rows([k + 1 for k in masks] + [1], R_SPL)
+    norm(done[2], strips)
+
     def own_cols(zz):
         return pl.ds(zz * ratio, ratio)
 
     def ow_slot_z(p):
         return owg.at[:, p, ow_piece(s), :]
 
+    def hand_over(k, j):
+        zz = flip(z, k)
+        push(
+            spread.at[zz * ratio + j], owg.at[j, z, ow_piece(s), :], S_OZ, one_r.at[R_OZ], to_head(k)
+        )
+
     with jax.named_scope("spread"):
         own_spread.wait()
-        arrived(spread.at[pl.ds(0, n_seq - 1)], one_r.at[R_SP])
-        own_ow = load(spread.at[own_cols(z)], ow_slot_z(z), 7)
-        for k in range(1, n_head):
-            push(spread.at[own_cols(flip(z, k))], ow_slot_z(z), S_OZ, one_r.at[R_OZ], to_head(k))
+        arrived(spread.at[pl.ds(0, n_chip - 1)], one_r.at[R_SP])
+        if ratio > 1:
+            for j in range(0, ratio, 2):
+                for k in range(1, n_head):
+                    hand_over(k, j + core)
 
     with jax.named_scope("relay2"):
         for half, b in second:
@@ -323,6 +336,9 @@
         for k in far:
             for half in range(2):
                 gather_relay(half_rows, half, k, S_QW, qw_r, qc_r)
+        if depth % LANES == 0:
+            for k in far:
+                queries[...] += shard_queries(flip(s, k), depth)
 
     @pl.when(core == 1)
     def _():
@@ -332,7 +348,7 @@
             key_normed = (key_sum[...] / jnp.sqrt(k_mean + 1e-06) * kg[...]).astype(BF16)
             for q in range(2):
                 kall[2 * chip + q] = key_normed[q * text : (q + 1) * text]
-            spread_text(kall, S_K, R_K)
+            spread_text(kall, R_K)
         with jax.named_scope("v_sum"):
             arrived(cvr.at[pl.ds(0, n_seq - 1)], one_r.at[R_CV])
             both = [cvr[0].astype(F32), own_v[...]]
@@ -340,7 +356,7 @@
                 for c in range(1, n_chip):
                     both[q] = both[q] + cvr[q * n_chip + c].astype(F32)
                 vall[2 * chip + q] = both[q].astype(BF16)
-            spread_text(vall, S_V, R_V)
+            spread_text(vall, R_V)
 
     def ow_half(half, p):
         if ratio == 1:
@@ -354,8 +370,6 @@
 
     with jax.named_scope("q_far"):
         for k in far:
-            if depth % LANES == 0:
-                queries[...] += shard_queries(flip(s, k), depth)
             arrived(shard_rows(flip(s, k + 1)), qc_r.at[k // 2])
             if depth % LANES == 0:
                 queries[...] += shard_queries(flip(s, k + 1), depth)
@@ -366,27 +380,30 @@
         for k in range(1, n_head):
             push(qsq.at[0], qsq.at[k], S_QSQ, one_r.at[R_QSQ], to_head(k))
 
+    with jax.named_scope("spread_late"):
+        arrived(spread.at[pl.ds(0, n_chip)], one_r.at[R_SPL])
+        own_ow = load(spread.at[own_cols(z)], ow_slot_z(z), 3)
+        for k in range(1, n_head):
+            if ratio > 1:
+                for j in range(0, ratio, 2):
+                    hand_over(k, j + 1 - core)
+            else:
+                hand_over(k, 0)
+
     @pl.when(core == 1)
     def _():
         with jax.named_scope("kv_in"):
-            for ref, group, chips in ((kall, S_K, R_K), (vall, S_V, R_V)):
+            for ref, chips in ((kall, R_K), (vall, R_V)):
                 arrived(ref.at[pl.ds(0, n_seq - 2)], one_r.at[chips])
                 for k in masks:
                     here = chip_slot(ref, flip(chip, k // 2))
-                    push(here, here, group, one_r.at[chips + 1], to_seq(1))
+                    push(here, here, S_KV, one_r.at[chips + 1], to_seq(1))
 
     @pl.when(core == 0)
     def _():
         with jax.named_scope("kv_end"):
             for ref, chips in ((kall, R_K), (vall, R_V)):
                 arrived(ref, one_r.at[chips + 1])
-
-    with jax.named_scope("ow_start"):
-        own_ow.wait()
-        arrived(owg.at[:, pl.ds(0, n_head - 1), ow_piece(s), :], one_r.at[R_OZ])
-        for half, b in first + second:
-            gather_own(ow_half, half, [b], S_OG, og_r)
-        gather_core(ow_half, S_OG, oc_r)
 
     with jax.named_scope("q_norm"):
         arrived(qsq.at[pl.ds(1, n_head - 1)], one_r.at[R_QSQ])
@@ -424,6 +441,14 @@
     def ow_relays(pairs):
         for half, b in pairs:
             gather_relay(ow_half, half, b, S_OG, og_r, oc_r)
+
+    def ow_begin():
+        with jax.named_scope("ow_start"):
+            own_ow.wait()
+            arrived(owg.at[:, pl.ds(0, n_head - 1), ow_piece(s), :], one_r.at[R_OZ])
+            for half, b in first + second:
+                gather_own(ow_half, half, [b], S_OG, og_r)
+            gather_core(ow_half, S_OG, oc_r)
 
     all_text = n_seq * text
     with jax.named_scope("attend"):
@@ -447,6 +472,8 @@
                 ).astype(BF16)
             for way in (1, -1):
                 reach(way, c, 1)
+            if c == 1:
+                ow_begin()
 
     cols = owg.shape[3]
     part_width = mod_out.shape[1]
@@ -496,8 +523,7 @@
     accumulate(3, chunks)
     with jax.named_scope("left1"):
         few = pl.ds(0, n_chip - 1)
-        left(ctxg.at[few, ctx_rows(0)], send_sem.at[S_CTX])
-        left(ctxg.at[few, ctx_rows(0)], send_sem.at[S_CTZ])
+        left(ctxg.at[few], send_sem.at[S_CTX])
         left(kvw.at[0], send_sem.at[S_W])
         left(spread.at[pl.ds(0, n_seq - 1)], send_sem.at[S_SP])
         left(shard_rows(0, n_seq - 1), send_sem.at[S_QW])
@@ -514,8 +540,7 @@
             left(ckr.at[few], send_sem.at[S_CK])
             left(cvr.at[few], send_sem.at[S_CV])
             left(ksq.at[pl.ds(0, n_head - 1)], send_sem.at[S_KSQ])
-            for group in (S_V, S_K):
-                left(qwg.at[pl.ds(0, 2 * (n_seq - 1) * text)], send_sem.at[group])
+            left(qwg.at[pl.ds(0, 4 * (n_seq - 1) * text)], send_sem.at[S_KV])
 
     def modulate(c):
         at = cuts[c]
@@ -523,11 +548,11 @@
         with jax.named_scope(f"stat{c}"):
             arrived(stat.at[c, pl.ds(1, n_head - 1)], st_r.at[c])
         with jax.named_scope(f"modulate{c}"):
-            both = jnp.sum(stat[c], axis=0) / (part_width * n_head)
-            mean2 = both[:1]
-            inverse = 1.0 / jnp.sqrt(both[1:] - mean2 * mean2 + 1e-06)
-            mean_col = row_to_column(mean2, step)
-            inv_col = row_to_column(inverse, step)
+            wide_row = -(-2 * step // LANES) * LANES
+            both = jnp.sum(stat[c, :, :, :wide_row], axis=0) / (part_width * n_head)
+            both_col = row_to_column(both, 2 * step)
+            mean_col = both_col[:step]
+            inv_col = 1.0 / jnp.sqrt(both_col[step:] - mean_col * mean_col + 1e-06)
             wide = resid_out[at, :].astype(F32)
             mod_out[at, :] = (
                 (wide - mean_col) * inv_col * (1.0 + shsc[1, :1, :]) + shsc[0, :1, :]
@@ -549,8 +574,8 @@
                 wide = rounded.astype(F32)
                 row_sum = row_sum + jnp.sum(wide, axis=1, keepdims=True)
                 row_sq = row_sq + jnp.sum(wide * wide, axis=1, keepdims=True)
-            stat[c, 0, :1] = column_to_row(row_sum)
-            stat[c, 0, 1:] = column_to_row(row_sq)
+            moments = column_to_row(jnp.concatenate([row_sum, row_sq], axis=0))
+            stat[c, 0, :, : moments.shape[1]] = moments
             for k in range(1, n_head):
                 push(stat.at[c, 0], stat.at[c, k], S_ST, st_r.at[c], to_head(k))
     with jax.named_scope("left2"):
@@ -647,7 +672,7 @@
             pltpu.VMEM((tok, att), F32),
             pltpu.VMEM((n_head, 1, tok), F32),
             pltpu.VMEM((n_head, 1, -(-2 * text // LANES) * LANES), F32),
-            pltpu.VMEM((chunks, n_head, 2, -(-max(sizes) // LANES) * LANES), F32),
+            pltpu.VMEM((chunks, n_head, 1, -(-2 * max(sizes) // LANES) * LANES), F32),
             pltpu.VMEM((2, 8, part_width), F32),
             pltpu.VMEM(time_weight.shape, BF16),
             pltpu.VMEM((1, att), F32),
@@ -657,14 +682,14 @@
             pltpu.VMEM((tok, part_width), F32),
             pltpu.VMEM((1, 1), jnp.int32),
             pltpu.VMEM((1, 1), jnp.int32),
-            dma((14,)),
-            dma((14,)),
+            dma((13,)),
+            dma((12,)),
             dma((2, n_head - 1)),
-            *[dma((n_chip,))] * 2,
-            *[dma((2, n_chip)), dma((n_chip,))] * 2,
+            *[dma((n_chip - 1,))] * 2,
+            *[dma((2, n_chip - 1)), dma((n_chip,))] * 2,
             dma((chunks, n_head - 1)),
             dma((chunks,)),
-            dma((11,)),
+            dma((12,)),
         ],
         compiler_params=pltpu.CompilerParams(
             collective_id=0, has_side_effects=True, vmem_limit_bytes=VMEM_MOST - 2 * out_bytes

time: 62.3 us -> 60.6 us (0.973)
  Pallas kernels: 60.2 us -> 58.5 us
    pallas_call x1, Pallas kernels: 58.7 us -> 57 us  [on_device(): pl.pallas_call(functools.partial(body, n_seq, n_head, cuts, sliced), out_...]
where the time goes in v6:
time: 60.6 us; the launch traced here: 60.5 us
  Pallas kernels  58.5 us (97%)
  between operations  1.93 us (3%)
    pallas_call x1, Pallas kernels, on_device(): pl.pallas_call(functools.partial(body, n_seq, n_head, cuts, sliced), out_...  57 us
    pallas_call x1, Pallas kernels, on_device(): pl.pallas_call(put_out, out_shape=[jax.ShapeDtypeStruct((tok, part_width)...  1.55 us

profile of v6, /device:TPU:0, one launch (start us, length us, event | category | flops | bytes accessed | tf_op | source)
XLA Modules:
  0.0 60.5 jit_solution(11133730000834078138)
XLA Ops:
  1.9 57.0 %shard_map.140 = (bf16[512,1280]{1,0:T(8,128)(2,1)S(1)}, bf16[512,1280]{1,0:T(8,128)(2,1)S(1)}) custom-call(s32[1,1]{1,0:T(1,128)} %bitcast.4.refs_0_, s32[1,1]{1,0:T(1,128)} %bitcast.5.refs_1_, bf16[512,5120]{1,0:T(8,128)(2,1)} %refs_2_.1, bf16[64,5120]{1,0:T(8,128)(2,1)} %refs_3_.1, bf16[640,256]{1,0:T(8,128)(2,1)} %refs_4_.1, bf16[640,256]{1,0:T(8,128)(2,1)} %refs_5_.1, ...), custom_call_target="tpu_custom_call" | custom-call | tf_op jit(solution)/shard_map/pallas_call | solution.py:649
  58.9 1.5 %shard_map.141 = (bf16[512,1280]{1,0:T(8,128)(2,1)}, bf16[512,1280]{1,0:T(8,128)(2,1)}) custom-call(bf16[512,1280]{1,0:T(8,128)(2,1)S(1)} %get-tuple-element.4.resid, bf16[512,1280]{1,0:T(8,128)(2,1)S(1)} %get-tuple-element.5.mod), custom_call_target="tpu_custom_call" | custom-call | tf_op jit(solution)/shard_map/pallas_call | solution.py:713

commit v7 on v6

--- a/solution.py
+++ b/solution.py
@@ -472,8 +472,8 @@
                 ).astype(BF16)
             for way in (1, -1):
                 reach(way, c, 1)
-            if c == 1:
-                ow_begin()
+            if c < 2:
+                pl.when(core == c)(ow_begin)
 
     cols = owg.shape[3]
     part_width = mod_out.shape[1]

time: 60.6 us -> 62.4 us (1.030)
  Pallas kernels: 58.5 us -> 60.3 us
    pallas_call x1, Pallas kernels: 57 us -> 58.8 us  [on_device(): pl.pallas_call(functools.partial(body, n_seq, n_head, cuts, sliced), out_...]
where the time goes in v7:
time: 62.4 us; the launch traced here: 62.2 us
  Pallas kernels  60.3 us (97%)
  between operations  1.93 us (3%)
    pallas_call x1, Pallas kernels, on_device(): pl.pallas_call(functools.partial(body, n_seq, n_head, cuts, sliced), out_...  58.8 us
    pallas_call x1, Pallas kernels, on_device(): pl.pallas_call(put_out, out_shape=[jax.ShapeDtypeStruct((tok, part_width)...  1.55 us

profile of v7, /device:TPU:0, one launch (start us, length us, event | category | flops | bytes accessed | tf_op | source)
XLA Modules:
  0.0 62.2 jit_solution(15931659338862805819)
XLA Ops:
  1.9 58.8 %shard_map.140 = (bf16[512,1280]{1,0:T(8,128)(2,1)S(1)}, bf16[512,1280]{1,0:T(8,128)(2,1)S(1)}) custom-call(s32[1,1]{1,0:T(1,128)} %bitcast.4.refs_0_, s32[1,1]{1,0:T(1,128)} %bitcast.5.refs_1_, bf16[512,5120]{1,0:T(8,128)(2,1)} %refs_2_.1, bf16[64,5120]{1,0:T(8,128)(2,1)} %refs_3_.1, bf16[640,256]{1,0:T(8,128)(2,1)} %refs_4_.1, bf16[640,256]{1,0:T(8,128)(2,1)} %refs_5_.1, ...), custom_call_target="tpu_custom_call" | custom-call | tf_op jit(solution)/shard_map/pallas_call | solution.py:649
  60.7 1.5 %shard_map.141 = (bf16[512,1280]{1,0:T(8,128)(2,1)}, bf16[512,1280]{1,0:T(8,128)(2,1)}) custom-call(bf16[512,1280]{1,0:T(8,128)(2,1)S(1)} %get-tuple-element.4.resid, bf16[512,1280]{1,0:T(8,128)(2,1)S(1)} %get-tuple-element.5.mod), custom_call_target="tpu_custom_call" | custom-call | tf_op jit(solution)/shard_map/pallas_call | solution.py:713
